TPU v7x, 32 devices: a whole 2x2x4 slice. The times are simulated.
32 devices in a mesh: pass: 8 (over z, x), cell: 4 (over y, core).
Axes of the slice: x: 2, y: 2, z: 4, core: 2. Of those that a mesh axis runs over, the one named last changes fastest.
Arguments:
- flow_state: float32 [2048, 4096], P('pass', 'cell'), may hold values from -6 to 6
- face_weights: float32 [4, 2048, 4096], P(None, 'pass', 'cell'), may hold values from 0.02 to 0.24
- forcing: float32 [2048, 4096], P('pass', 'cell'), may hold values from -1.2 to 1.2
- lagged_planes: float32 [8, 8, 4096], P('pass', None, 'cell'), may hold values from -6 to 6
- phase_lag: int32 [4, 2], replicated, may hold values from 0 to 8
- face_map: int32 [8, 4096], P('pass', 'cell'), may hold values from 0 to 4095, as said below
- surface_record: bfloat16 [8, 120, 4096], P('pass', None, 'cell'), may hold values from -6 to 6
- face_radius: float32 [2, 4096], P(None, 'cell'), may hold values from 0.3 to 1
- face_angle: float32 [2, 4096], P(None, 'cell'), may hold values from -0.3 to 0.3
- face_axial: float32 [2, 4096], P(None, 'cell'), may hold values from -0.3 to 0.3
- face_stagger: float32 [2, 4096], P(None, 'cell'), may hold values from -1.2 to 1.2
- face_area: float32 [2, 4096], P(None, 'cell'), may hold values from 0.5 to 1.5
- listeners: float32 [3, 1024], replicated, as said below
- observer_group: int32 [1024], replicated, may hold values from 0 to 15
Outputs:
- final_field: float32 [2048, 4096], P('pass', 'cell')
- acoustic: float32 [1024, 128], P('cell')
- array_signal: float32 [16, 128], replicated
Inputs may be any that keep to these rules, and one draw needn't show every extreme that they name: face_map[j, a] lies in the aligned block of 1024 axial indices that holds a, and for each j the entries of a block are a permutation of that block. `listeners`: every observer is between 1.3 and 4 from the anchor.
All inputs are finite; a program needn't handle non-finite values.
Results may differ from a plain program's by a relative error of at most 0.0035.
Values sent between devices are 32-bit elements; how exact they have to be, the bound alone decides.
A program may use at most 64 MiB of HBM per device.

v0:
```python
import math
import jax
import jax.numpy as jnp
from jax import lax
from jax.sharding import PartitionSpec as P

STEPS = 8
GROUPS = 16
sound_speed = 2.0


def padded(shard, sides, width):
    for axis, dim in sides:
        devices, length = (lax.axis_size(axis), shard.shape[dim])
        up = [(i, (i + 1) % devices) for i in range(devices - 1)]
        down = [(j, i) for i, j in up]
        last = lax.slice_in_dim(shard, length - width, length, axis=dim)
        initial = lax.slice_in_dim(shard, 0, width, axis=dim)
        before = lax.ppermute(last, axis, up)
        after = lax.ppermute(initial, axis, down)
        shard = jnp.concatenate([before, shard, after], axis=dim)
    return shard


def shifted(block, axis, distance):
    devices = range(lax.axis_size(axis))
    route = [((i - distance) % len(devices), i) for i in devices]
    return lax.ppermute(block, axis, route)


def relax(field, coeff, forcing, ghost_low, ghost_high):
    edges = jnp.stack([field[:, 0], field[:, -1]], axis=0)
    rim = padded(edges, (("cell", 0),), 1)
    below = jnp.concatenate([ghost_low[None, :], field[:-1, :]], axis=0)
    above = jnp.concatenate([field[1:, :], ghost_high[None, :]], axis=0)
    left = jnp.concatenate([rim[0][:, None], field[:, :-1]], axis=1)
    right = jnp.concatenate([field[:, 1:], rim[3][:, None]], axis=1)
    keep = 1.0 - coeff[0] - coeff[1] - coeff[2] - coeff[3]
    return (
        keep * field
        + coeff[0] * below
        + coeff[1] * above
        + coeff[2] * left
        + coeff[3] * right
        + forcing
    )


def time_rate(signal, axis):
    values = signal.astype(jnp.float32)
    length = values.shape[axis]
    inner = (
        lax.slice_in_dim(values, 2, length, axis=axis)
        - lax.slice_in_dim(values, 0, length - 2, axis=axis)
    ) * 0.5
    head = lax.slice_in_dim(values, 1, 2, axis=axis) - lax.slice_in_dim(values, 0, 1, axis=axis)
    tail = lax.slice_in_dim(values, length - 1, length, axis=axis) - lax.slice_in_dim(
        values, length - 2, length - 1, axis=axis
    )
    return jnp.concatenate([head, inner, tail], axis=axis).astype(jnp.bfloat16)


def kernel_pair(points, theta, radius, angle, axial, stagger, area, scale):
    phase = theta + angle
    cos_phase = jnp.cos(phase)
    sin_phase = jnp.sin(phase)
    normal_x = -jnp.cos(stagger) * sin_phase
    normal_y = jnp.cos(stagger) * cos_phase
    normal_z = jnp.sin(stagger)
    delta_x = points[0][:, None] - (radius * cos_phase)[None, :]
    delta_y = points[1][:, None] - (radius * sin_phase)[None, :]
    delta_z = points[2][:, None] - axial[None, :]
    dist_sq = delta_x * delta_x + delta_y * delta_y + delta_z * delta_z
    dist = jnp.sqrt(dist_sq)
    cosine = (
        normal_x[None, :] * delta_x + normal_y[None, :] * delta_y + normal_z[None, :] * delta_z
    ) / dist
    weight = (area * scale / (4.0 * math.pi))[None, :] * cosine
    press = (weight / dist_sq).astype(jnp.bfloat16)
    change = (weight / (sound_speed * dist)).astype(jnp.bfloat16)
    return jnp.concatenate([press, change], axis=1)


def on_device(
    flow_state,
    face_weights,
    forcing,
    lagged_planes,
    phase_lag,
    face_map,
    surface_record,
    face_radius,
    face_angle,
    face_axial,
    face_stagger,
    face_area,
    listeners,
    observer_group,
):
    passes = lax.axis_size("pass")
    cells = lax.axis_size("cell")
    pass_index = lax.axis_index("pass")
    cell_index = lax.axis_index("cell")
    passage_count = passes // 2
    half = pass_index % 2
    passage = pass_index // 2
    field = flow_state
    height = field.shape[0]
    width = field.shape[1]
    lower_levels = jnp.concatenate([field[None, 0, :], lagged_planes[0]], axis=0)
    upper_levels = jnp.concatenate([field[None, -1, :], lagged_planes[0]], axis=0)
    local_map = face_map[0] - cell_index * width
    after_lag = phase_lag[(passage + 1) % passage_count, 0]
    before_lag = phase_lag[(passage + passage_count - 1) % passage_count, 1]
    surfaces = []
    for level in range(STEPS):
        up_pick = jnp.where(half == 1, after_lag, 0)
        down_pick = jnp.where(half == 0, before_lag, 0)
        raw_low = shifted(upper_levels[up_pick], "pass", 1)
        raw_high = shifted(lower_levels[down_pick], "pass", -1)
        mapped = jnp.take(jnp.where(half == 0, raw_low, raw_high), local_map)
        ghost_low = jnp.where(half == 0, mapped, raw_low)
        ghost_high = jnp.where(half == 1, mapped, raw_high)
        field = relax(field, face_weights, forcing, ghost_low, ghost_high)
        lower_levels = jnp.concatenate([field[None, 0, :], lower_levels[:-1]], axis=0)
        upper_levels = jnp.concatenate([field[None, -1, :], upper_levels[:-1]], axis=0)
        surfaces.append(field[height // 2].astype(jnp.bfloat16))
    surface = jnp.concatenate([surface_record[0], jnp.stack(surfaces, axis=0)], axis=0)
    rate = time_rate(surface, 0)
    data = jnp.concatenate([surface, rate], axis=1)
    theta = passage.astype(jnp.float32) * (2.0 * math.pi / passage_count)
    scale = 64.0 / math.sqrt(width * cells * passes)
    radius = face_radius[half]
    angle = face_angle[half]
    axial = face_axial[half]
    stagger = face_stagger[half]
    area = face_area[half]
    per_cell = listeners.shape[1] // cells
    block = math.gcd(per_cell * lax.axis_size("cell"), 256)

    def one_block(offset):
        rows = offset * block + jnp.arange(block, dtype=jnp.int32)
        points = jnp.take(listeners, rows, axis=1)
        kernel = kernel_pair(points, theta, radius, angle, axial, stagger, area, scale)
        return lax.dot_general(
            kernel, data, (((1,), (1,)), ((), ())), preferred_element_type=jnp.float32
        )

    blocks = lax.map(
        one_block, jnp.arange(per_cell * lax.axis_size("cell") // block, dtype=jnp.int32)
    )
    share = lax.psum_scatter(
        blocks.reshape(per_cell * lax.axis_size("cell"), blocks.shape[-1]),
        "cell",
        scatter_dimension=0,
        tiled=True,
    )
    acoustic = lax.psum(share, "pass")
    labels = jnp.arange(GROUPS, dtype=jnp.int32)
    my_groups = lax.dynamic_slice_in_dim(observer_group, cell_index * per_cell, per_cell)
    member = (my_groups[None, :] == labels[:, None]).astype(jnp.float32)
    counts = jnp.sum((observer_group[None, :] == labels[:, None]).astype(jnp.float32), axis=1)
    partial_totals = jnp.dot(
        member, acoustic, precision=lax.Precision.HIGHEST, preferred_element_type=jnp.float32
    )
    totals = lax.psum(partial_totals, "cell")
    array_signal = totals / jnp.maximum(counts, 1.0)[:, None]
    return (field, acoustic, array_signal)


def solution(mesh):
    return jax.shard_map(
        on_device,
        mesh=mesh,
        in_specs=(
            P("pass", "cell"),
            P(None, "pass", "cell"),
            P("pass", "cell"),
            P("pass", None, "cell"),
            P(),
            P("pass", "cell"),
            P("pass", None, "cell"),
            P(None, "cell"),
            P(None, "cell"),
            P(None, "cell"),
            P(None, "cell"),
            P(None, "cell"),
            P(),
            P(),
        ),
        out_specs=(P("pass", "cell"), P("cell", None), P()),
        check_vma=False,
    )
```

profile of v0, /device:TPU:0, one launch (start us, length us, event | category | flops | bytes accessed | tf_op | source)
XLA Modules:
  0.0 348.3 jit_solution(7912482702422968674)
XLA Ops:
  8.5 2.4 collective-permute-start.2
  10.9 1.3 collective-permute-start.3
  12.2 1.3 constant_dynamic-slice_fusion.12
  16.5 2.4 collective-permute-start
  18.9 3.1 collective-permute-start.1
  22.1 3.2 fusion.109
  25.3 1.7 fusion.108
  28.6 4.5 %gather_fusion.1 = f32[1024]{0:T(1024)S(1)} fusion(f32[1024]{0:T(1024)S(1)} %broadcast_select_fusion.7, s32[1024]{0:T(1024)S(1)} %fusion.82), kind=kCustom, calls=%fused_computation.clone | custom fusion | bytes 12288 | tf_op jit(solution)/shard_map/jit(_take)/gather | solution.py:121
  33.2 5.1 %fusion.22 = (f32[256,1024]{1,0:T(8,128)S(1)}, f32[256,1024]{1,0:T(8,128)S(1)}) fusion(f32[256,1024]{1,0:T(8,128)S(1)} %copy-done, f32[255,1024]{1,0:T(8,128)} %get-tuple-element.332, f32[1,1024]{1,0:T(1,128)S(1)} %bitcast.169, f32[1,1024]{1,0:T(1,128)S(1)} %bitcast.172, f32[255,1024]{1,0:T(8,128)} %get-tuple-element.331, ...), kind=kLoop, calls=%fused_computation.51 | loop fusion | flops 4718592 | bytes 12582912 | tf_op jit(solution)/shard_map/add | solution.py:40
  38.5 1.5 fusion.106
  40.0 4.0 %collective-permute-start.6 = (f32[1,256]{1,0:T(1,128)S(1)}, f32[1,256]{1,0:T(1,128)S(1)}, u32[]{:S(2)}, u32[]{:S(2)}) collective-permute-start(f32[1,256]{1,0:T(1,128)S(1)} %bitcast.206), channel_id=1, source_target_pairs={{0,1},{1,2},{2,3},{4,5},{5,6},{6,7},{8,9},{9,10},{10,11},{12,13},{... | collective-permute-start | bytes 3080 | tf_op jit(solution)/shard_map/ppermute | solution.py:19
  44.0 1.3 collective-permute-start.7
  45.5 4.7 %collective-permute-start.5 = (f32[1024]{0:T(1024)S(1)}, f32[1024]{0:T(1024)S(1)}, u32[]{:S(2)}, u32[]{:S(2)}) collective-permute-start(f32[1024]{0:T(1024)S(1)} %bitcast.189), channel_id=1, source_target_pairs={{4,0},{8,4},{12,8},{16,12},{20,16},{24,20},{28,24},{0,28},{5,1},{9... | collective-permute-start | bytes 12296 | tf_op jit(solution)/shard_map/ppermute | solution.py:28
  50.2 1.7 fusion.105
  52.2 4.5 %gather_fusion.2 = f32[1024]{0:T(1024)S(1)} fusion(f32[1024]{0:T(1024)S(1)} %broadcast_select_fusion.6, s32[1024]{0:T(1024)S(1)} %fusion.82), kind=kCustom, calls=%fused_computation.2.clone | custom fusion | bytes 12288 | tf_op jit(solution)/shard_map/jit(_take)/gather | solution.py:121
  56.8 4.8 %fusion.27 = f32[256,1024]{1,0:T(8,128)S(1)} fusion(f32[256,1024]{1,0:T(8,128)S(1)} %copy-done, f32[255,1024]{1,0:T(8,128)} %get-tuple-element.326, f32[1,1024]{1,0:T(1,128)S(1)} %bitcast.174, f32[1,1024]{1,0:T(1,128)S(1)} %bitcast.173, f32[255,1024]{1,0:T(8,128)} %get-tuple-element.325, f32[256,1023]{1,0:T(8,128)} %get-tuple-element.324, ...), kind=kLoop, calls=%fused_computation.60 | loop fusion | flops 3670016 | bytes 12582912 | tf_op jit(solution)/shard_map/add | solution.py:40
  61.8 1.5 fusion.103
  63.3 4.1 %collective-permute-start.10 = (f32[1,256]{1,0:T(1,128)S(1)}, f32[1,256]{1,0:T(1,128)S(1)}, u32[]{:S(2)}, u32[]{:S(2)}) collective-permute-start(f32[1,256]{1,0:T(1,128)S(1)} %bitcast.216), channel_id=1, source_target_pairs={{0,1},{1,2},{2,3},{4,5},{5,6},{6,7},{8,9},{9,10},{10,11},{12,13},{... | collective-permute-start | bytes 3080 | tf_op jit(solution)/shard_map/ppermute | solution.py:19
  67.4 1.3 collective-permute-start.11
  68.8 4.8 %collective-permute-start.9 = (f32[1024]{0:T(1024)S(1)}, f32[1024]{0:T(1024)S(1)}, u32[]{:S(2)}, u32[]{:S(2)}) collective-permute-start(f32[1024]{0:T(1024)S(1)} %bitcast.198), channel_id=1, source_target_pairs={{4,0},{8,4},{12,8},{16,12},{20,16},{24,20},{28,24},{0,28},{5,1},{9... | collective-permute-start | bytes 12296 | tf_op jit(solution)/shard_map/ppermute | solution.py:28
  73.6 1.7 fusion.102
  75.6 4.5 %gather_fusion.3 = f32[1024]{0:T(1024)S(1)} fusion(f32[1024]{0:T(1024)S(1)} %broadcast_select_fusion.5, s32[1024]{0:T(1024)S(1)} %fusion.82), kind=kCustom, calls=%fused_computation.3.clone | custom fusion | bytes 12288 | tf_op jit(solution)/shard_map/jit(_take)/gather | solution.py:121
  80.1 5.1 %fusion.32 = f32[256,1024]{1,0:T(8,128)S(1)} fusion(f32[256,1024]{1,0:T(8,128)S(1)} %copy-done, f32[255,1024]{1,0:T(8,128)} %get-tuple-element.320, f32[1,1024]{1,0:T(1,128)S(1)} %bitcast.176, f32[1,1024]{1,0:T(1,128)S(1)} %bitcast.175, f32[255,1024]{1,0:T(8,128)} %get-tuple-element.319, f32[256,1023]{1,0:T(8,128)} %get-tuple-element.318, ...), kind=kLoop, calls=%fused_computation.69 | loop fusion | flops 3670016 | bytes 12582912 | tf_op jit(solution)/shard_map/add | solution.py:40
  85.4 1.5 fusion.100
  86.9 4.3 %collective-permute-start.14 = (f32[1,256]{1,0:T(1,128)S(1)}, f32[1,256]{1,0:T(1,128)S(1)}, u32[]{:S(2)}, u32[]{:S(2)}) collective-permute-start(f32[1,256]{1,0:T(1,128)S(1)} %bitcast.205), channel_id=1, source_target_pairs={{0,1},{1,2},{2,3},{4,5},{5,6},{6,7},{8,9},{9,10},{10,11},{12,13},{... | collective-permute-start | bytes 3080 | tf_op jit(solution)/shard_map/ppermute | solution.py:19
  92.6 4.7 %collective-permute-start.13 = (f32[1024]{0:T(1024)S(1)}, f32[1024]{0:T(1024)S(1)}, u32[]{:S(2)}, u32[]{:S(2)}) collective-permute-start(f32[1024]{0:T(1024)S(1)} %bitcast.190), channel_id=1, source_target_pairs={{4,0},{8,4},{12,8},{16,12},{20,16},{24,20},{28,24},{0,28},{5,1},{9... | collective-permute-start | bytes 12296 | tf_op jit(solution)/shard_map/ppermute | solution.py:28
  97.3 1.7 fusion.99
  99.4 4.5 %gather_fusion.4 = f32[1024]{0:T(1024)S(1)} fusion(f32[1024]{0:T(1024)S(1)} %broadcast_select_fusion.4, s32[1024]{0:T(1024)S(1)} %fusion.82), kind=kCustom, calls=%fused_computation.4.clone | custom fusion | bytes 12288 | tf_op jit(solution)/shard_map/jit(_take)/gather | solution.py:121
  103.9 4.8 %fusion.37 = f32[256,1024]{1,0:T(8,128)S(1)} fusion(f32[256,1024]{1,0:T(8,128)S(1)} %copy-done, f32[255,1024]{1,0:T(8,128)} %get-tuple-element.314, f32[1,1024]{1,0:T(1,128)S(1)} %bitcast.178, f32[1,1024]{1,0:T(1,128)S(1)} %bitcast.177, f32[255,1024]{1,0:T(8,128)} %get-tuple-element.313, f32[256,1023]{1,0:T(8,128)} %get-tuple-element.312, ...), kind=kLoop, calls=%fused_computation.78 | loop fusion | flops 3670016 | bytes 12582912 | tf_op jit(solution)/shard_map/add | solution.py:40
  108.9 1.5 fusion.97
  110.4 4.4 %collective-permute-start.18 = (f32[1,256]{1,0:T(1,128)S(1)}, f32[1,256]{1,0:T(1,128)S(1)}, u32[]{:S(2)}, u32[]{:S(2)}) collective-permute-start(f32[1,256]{1,0:T(1,128)S(1)} %bitcast.217), channel_id=1, source_target_pairs={{0,1},{1,2},{2,3},{4,5},{5,6},{6,7},{8,9},{9,10},{10,11},{12,13},{... | collective-permute-start | bytes 3080 | tf_op jit(solution)/shard_map/ppermute | solution.py:19
  114.8 1.3 collective-permute-start.19
  116.2 4.8 %collective-permute-start.17 = (f32[1024]{0:T(1024)S(1)}, f32[1024]{0:T(1024)S(1)}, u32[]{:S(2)}, u32[]{:S(2)}) collective-permute-start(f32[1024]{0:T(1024)S(1)} %bitcast.199), channel_id=1, source_target_pairs={{4,0},{8,4},{12,8},{16,12},{20,16},{24,20},{28,24},{0,28},{5,1},{9... | collective-permute-start | bytes 12296 | tf_op jit(solution)/shard_map/ppermute | solution.py:28
  121.0 1.7 fusion.96
  123.0 4.5 %gather_fusion.5 = f32[1024]{0:T(1024)S(1)} fusion(f32[1024]{0:T(1024)S(1)} %broadcast_select_fusion.3, s32[1024]{0:T(1024)S(1)} %fusion.82), kind=kCustom, calls=%fused_computation.5.clone | custom fusion | bytes 12288 | tf_op jit(solution)/shard_map/jit(_take)/gather | solution.py:121
  127.5 5.1 %fusion.42 = f32[256,1024]{1,0:T(8,128)S(1)} fusion(f32[256,1024]{1,0:T(8,128)S(1)} %copy-done, f32[255,1024]{1,0:T(8,128)} %get-tuple-element.308, f32[1,1024]{1,0:T(1,128)S(1)} %bitcast.180, f32[1,1024]{1,0:T(1,128)S(1)} %bitcast.179, f32[255,1024]{1,0:T(8,128)} %get-tuple-element.307, f32[256,1023]{1,0:T(8,128)} %get-tuple-element.306, ...), kind=kLoop, calls=%fused_computation.87 | loop fusion | flops 3670016 | bytes 12582912 | tf_op jit(solution)/shard_map/add | solution.py:40
  132.8 1.5 fusion.94
  134.3 4.2 %collective-permute-start.22 = (f32[1,256]{1,0:T(1,128)S(1)}, f32[1,256]{1,0:T(1,128)S(1)}, u32[]{:S(2)}, u32[]{:S(2)}) collective-permute-start(f32[1,256]{1,0:T(1,128)S(1)} %bitcast.207), channel_id=1, source_target_pairs={{0,1},{1,2},{2,3},{4,5},{5,6},{6,7},{8,9},{9,10},{10,11},{12,13},{... | collective-permute-start | bytes 3080 | tf_op jit(solution)/shard_map/ppermute | solution.py:19
  139.8 3.5 collective-permute-start.21
  143.4 1.7 fusion.93
  145.4 4.3 %collective-permute-done.20 = f32[1024]{0:T(1024)S(1)} collective-permute-done((f32[1024]{0:T(1024)S(1)}, f32[1024]{0:T(1024)S(1)}, u32[]{:S(2)}, u32[]{:S(2)}) %collective-permute-start.20) | collective-permute-done | bytes 4128 | tf_op jit(solution)/shard_map/ppermute | solution.py:28
  149.7 4.5 %gather_fusion.6 = f32[1024]{0:T(1024)S(1)} fusion(f32[1024]{0:T(1024)S(1)} %broadcast_select_fusion.2, s32[1024]{0:T(1024)S(1)} %fusion.82), kind=kCustom, calls=%fused_computation.6.clone | custom fusion | bytes 12288 | tf_op jit(solution)/shard_map/jit(_take)/gather | solution.py:121
  154.3 4.8 %fusion.47 = f32[256,1024]{1,0:T(8,128)S(1)} fusion(f32[256,1024]{1,0:T(8,128)S(1)} %copy-done, f32[255,1024]{1,0:T(8,128)} %get-tuple-element.302, f32[1,1024]{1,0:T(1,128)S(1)} %bitcast.182, f32[1,1024]{1,0:T(1,128)S(1)} %bitcast.181, f32[255,1024]{1,0:T(8,128)} %get-tuple-element.301, f32[256,1023]{1,0:T(8,128)} %get-tuple-element.300, ...), kind=kLoop, calls=%fused_computation.96 | loop fusion | flops 3670016 | bytes 12582912 | tf_op jit(solution)/shard_map/add | solution.py:40
  159.3 1.5 fusion.91
  160.8 4.3 %collective-permute-start.26 = (f32[1,256]{1,0:T(1,128)S(1)}, f32[1,256]{1,0:T(1,128)S(1)}, u32[]{:S(2)}, u32[]{:S(2)}) collective-permute-start(f32[1,256]{1,0:T(1,128)S(1)} %bitcast.218), channel_id=1, source_target_pairs={{0,1},{1,2},{2,3},{4,5},{5,6},{6,7},{8,9},{9,10},{10,11},{12,13},{... | collective-permute-start | bytes 3080 | tf_op jit(solution)/shard_map/ppermute | solution.py:19
  166.5 4.8 %collective-permute-start.25 = (f32[1024]{0:T(1024)S(1)}, f32[1024]{0:T(1024)S(1)}, u32[]{:S(2)}, u32[]{:S(2)}) collective-permute-start(f32[1024]{0:T(1024)S(1)} %bitcast.200), channel_id=1, source_target_pairs={{4,0},{8,4},{12,8},{16,12},{20,16},{24,20},{28,24},{0,28},{5,1},{9... | collective-permute-start | bytes 12296 | tf_op jit(solution)/shard_map/ppermute | solution.py:28
  171.2 1.7 fusion.90
  173.2 4.5 %gather_fusion.7 = f32[1024]{0:T(1024)S(1)} fusion(f32[1024]{0:T(1024)S(1)} %broadcast_select_fusion.1, s32[1024]{0:T(1024)S(1)} %fusion.82), kind=kCustom, calls=%fused_computation.7.clone | custom fusion | bytes 12288 | tf_op jit(solution)/shard_map/jit(_take)/gather | solution.py:121
  177.8 5.1 %fusion.52 = f32[256,1024]{1,0:T(8,128)S(1)} fusion(f32[256,1024]{1,0:T(8,128)S(1)} %copy-done, f32[255,1024]{1,0:T(8,128)} %get-tuple-element.296, f32[1,1024]{1,0:T(1,128)S(1)} %bitcast.184, f32[1,1024]{1,0:T(1,128)S(1)} %bitcast.183, f32[255,1024]{1,0:T(8,128)} %get-tuple-element.295, f32[256,1023]{1,0:T(8,128)} %get-tuple-element.294, ...), kind=kLoop, calls=%fused_computation.105 | loop fusion | flops 3670016 | bytes 12582912 | tf_op jit(solution)/shard_map/add | solution.py:40
  183.1 1.5 fusion.88
  184.6 5.1 %collective-permute-start.30 = (f32[1,256]{1,0:T(1,128)S(1)}, f32[1,256]{1,0:T(1,128)S(1)}, u32[]{:S(2)}, u32[]{:S(2)}) collective-permute-start(f32[1,256]{1,0:T(1,128)S(1)} %bitcast.210), channel_id=1, source_target_pairs={{0,1},{1,2},{2,3},{4,5},{5,6},{6,7},{8,9},{9,10},{10,11},{12,13},{... | collective-permute-start | bytes 3080 | tf_op jit(solution)/shard_map/ppermute | solution.py:19
  191.2 4.7 %collective-permute-start.29 = (f32[1024]{0:T(1024)S(1)}, f32[1024]{0:T(1024)S(1)}, u32[]{:S(2)}, u32[]{:S(2)}) collective-permute-start(f32[1024]{0:T(1024)S(1)} %bitcast.188), channel_id=1, source_target_pairs={{4,0},{8,4},{12,8},{16,12},{20,16},{24,20},{28,24},{0,28},{5,1},{9... | collective-permute-start | bytes 12296 | tf_op jit(solution)/shard_map/ppermute | solution.py:28
  195.9 1.7 fusion.87
  197.9 4.5 %gather_fusion.8 = f32[1024]{0:T(1024)S(1)} fusion(f32[1024]{0:T(1024)S(1)} %broadcast_select_fusion, s32[1024]{0:T(1024)S(1)} %fusion.82), kind=kCustom, calls=%fused_computation.8.clone | custom fusion | bytes 12288 | tf_op jit(solution)/shard_map/jit(_take)/gather | solution.py:121
  202.4 4.8 %fusion.57 = f32[256,1024]{1,0:T(8,128)S(1)} fusion(f32[256,1024]{1,0:T(8,128)S(1)} %copy-done, f32[255,1024]{1,0:T(8,128)} %get-tuple-element.290, f32[1,1024]{1,0:T(1,128)S(1)} %bitcast.171, f32[1,1024]{1,0:T(1,128)S(1)} %bitcast.170, f32[255,1024]{1,0:T(8,128)} %get-tuple-element.289, f32[256,1023]{1,0:T(8,128)} %get-tuple-element.288, ...), kind=kLoop, calls=%fused_computation.114 | loop fusion | flops 3670016 | bytes 12582912 | tf_op jit(solution)/shard_map/add | solution.py:40
  209.5 23.1 %while.13 = (s32[]{:T(128)}, f32[4,256,128]{2,1,0:T(8,128)}, f32[1024]{0:T(1024)S(1)}, f32[1,1024]{1,0:T(1,128)S(1)}, f32[]{:T(128)}, /*index=5*/f32[1024]{0:T(1...) while((s32[]{:T(128)}, f32[4,256,128]{2,1,0:T(8,128)}, ...), condition=%wide.region_1.3_spmd, body=%wide.region_0.2_spmd.sunk | while | flops 141568512 | bytes 2851517 | solution.py:149
  211.0 1.8 gather_fusion
  216.7 1.8 gather_fusion
  222.5 1.8 gather_fusion
  228.3 1.8 gather_fusion
  232.9 25.6 %reduce-scatter.2.cloned.1.call-done = f32[256,128]{1,0:T(8,128)} async-done(((f32[1024,128]{1,0:T(8,128)}), f32[256,128]{1,0:T(8,128)}) %reduce-scatter.2.cloned.1.call-update) | async-done | bytes 131088 | tf_op jit(solution)/shard_map/reduce_scatter | solution.py:152
  258.5 73.9 %all-reduce.2.cloned.1.call-done = f32[256,128]{1,0:T(8,128)} async-done(((f32[256,128]{1,0:T(8,128)}), f32[256,128]{1,0:T(8,128)}) %all-reduce.2.cloned.1.call-update) | async-done | bytes 131088 | tf_op jit(solution)/shard_map/psum | solution.py:158
  333.5 5.8 %psum.15 = f32[16,128]{1,0:T(8,128)S(1)} all-reduce(f32[16,128]{1,0:T(8,128)S(1)} %fusion.66), channel_id=1, replica_groups=mesh['pass'=8,'cell'=4] {'cell'}, use_global_device_ids=true, to_apply=%region_4.6 | all-reduce | flops 2048 | bytes 16384 | tf_op jit(solution)/shard_map/psum | solution.py:166
  339.9 1.6 copy.60
  (212 shorter events, 31.5 us)
Async XLA Ops:
  7.2 18.1 %copy-start.4 = (f32[256,1024]{1,0:T(8,128)S(1)}, f32[256,1024]{1,0:T(8,128)}, u32[]{:S(2)}) copy-start(f32[256,1024]{1,0:T(8,128)} %param.18) | copy-start | bytes 3145732
  7.2 251.3 %reduce-scatter.2.cloned.1.call-start = ((), (), s32[]{:S(2)}) async-start(), calls=%async_computation.1 | async-start | bytes 655360 | tf_op jit(solution)/shard_map/reduce_scatter | solution.py:152
  8.5 20.0 %collective-permute-start.2 = (f32[1,256]{1,0:T(1,128)S(1)}, f32[1,256]{1,0:T(1,128)S(1)}, u32[]{:S(2)}, u32[]{:S(2)}) collective-permute-start(f32[1,256]{1,0:T(1,128)S(1)} %bitcast.202), channel_id=1, source_target_pairs={{0,1},{1,2},{2,3},{4,5},{5,6},{6,7},{8,9},{9,10},{10,11},{12,13},{... | collective-permute-start | bytes 3080 | tf_op jit(solution)/shard_map/ppermute | solution.py:19
  10.9 17.4 %collective-permute-start.3 = (f32[1,256]{1,0:T(1,128)S(1)}, f32[1,256]{1,0:T(1,128)S(1)}, u32[]{:S(2)}, u32[]{:S(2)}) collective-permute-start(f32[1,256]{1,0:T(1,128)S(1)} %bitcast.203), channel_id=1, source_target_pairs={{1,0},{2,1},{3,2},{5,4},{6,5},{7,6},{9,8},{10,9},{11,10},{13,12},{... | collective-permute-start | bytes 3080 | tf_op jit(solution)/shard_map/ppermute | solution.py:20
  16.5 12.0 %collective-permute-start = (f32[1024]{0:T(1024)S(1)}, f32[1024]{0:T(1024)S(1)}, u32[]{:S(2)}, u32[]{:S(2)}) collective-permute-start(f32[1024]{0:T(1024)S(1)} %bitcast.186), channel_id=1, source_target_pairs={{28,0},{0,4},{4,8},{8,12},{12,16},{16,20},{20,24},{24,28},{29,1},{... | collective-permute-start | bytes 12296 | tf_op jit(solution)/shard_map/ppermute | solution.py:28
  18.9 9.7 %collective-permute-start.1 = (f32[1024]{0:T(1024)S(1)}, f32[1024]{0:T(1024)S(1)}, u32[]{:S(2)}, u32[]{:S(2)}) collective-permute-start(f32[1024]{0:T(1024)S(1)} %bitcast.185), channel_id=1, source_target_pairs={{4,0},{8,4},{12,8},{16,12},{20,16},{24,20},{28,24},{0,28},{5,1},{9... | collective-permute-start | bytes 12296 | tf_op jit(solution)/shard_map/ppermute | solution.py:28
  22.0 5.0 %copy-start.9 = (s32[1,1024]{1,0:T(1,128)S(1)}, s32[1,1024]{1,0:T(1,128)}, u32[]{:S(2)}) copy-start(s32[1,1024]{1,0:T(1,128)} %param.23) | copy-start | bytes 12292
  22.0 5.0 %copy-start.10 = (f32[2,1024]{1,0:T(2,128)S(1)}, f32[2,1024]{1,0:T(2,128)}, u32[]{:S(2)}) copy-start(f32[2,1024]{1,0:T(2,128)} %param.28) | copy-start | bytes 24580
  22.0 5.1 %copy-start.11 = (f32[2,1024]{1,0:T(2,128)S(1)}, f32[2,1024]{1,0:T(2,128)}, u32[]{:S(2)}) copy-start(f32[2,1024]{1,0:T(2,128)} %param.27) | copy-start | bytes 24580
  22.0 5.1 %copy-start.12 = (f32[2,1024]{1,0:T(2,128)S(1)}, f32[2,1024]{1,0:T(2,128)}, u32[]{:S(2)}) copy-start(f32[2,1024]{1,0:T(2,128)} %param.25) | copy-start | bytes 24580
  22.0 5.2 %copy-start.13 = (f32[2,1024]{1,0:T(2,128)S(1)}, f32[2,1024]{1,0:T(2,128)}, u32[]{:S(2)}) copy-start(f32[2,1024]{1,0:T(2,128)} %param.26) | copy-start | bytes 24580
  22.0 5.2 %copy-start.14 = (f32[2,1024]{1,0:T(2,128)S(1)}, f32[2,1024]{1,0:T(2,128)}, u32[]{:S(2)}) copy-start(f32[2,1024]{1,0:T(2,128)} %param.29) | copy-start | bytes 24580
  22.0 5.2 %copy-start.7 = (f32[3,1024]{1,0:T(4,128)S(1)}, f32[3,1024]{1,0:T(4,128)}, u32[]{:S(2)}) copy-start(f32[3,1024]{1,0:T(4,128)} %param.30) | copy-start | bytes 36868
  25.3 7.9 %copy-start = (f32[256,1024]{1,0:T(8,128)S(1)}, f32[256,1024]{1,0:T(8,128)}, u32[]{:S(2)}) copy-start(f32[256,1024]{1,0:T(8,128)} %param.20) | copy-start | bytes 3145732
  38.3 7.1 %copy-start.6 = (f32[1,8,1024]{2,1,0:T(8,128)S(1)}, f32[1,8,1024]{2,1,0:T(8,128)}, u32[]{:S(2)}) copy-start(f32[1,8,1024]{2,1,0:T(8,128)} %param.21) | copy-start | bytes 98308
  40.0 12.1 %collective-permute-start.6 = (f32[1,256]{1,0:T(1,128)S(1)}, f32[1,256]{1,0:T(1,128)S(1)}, u32[]{:S(2)}, u32[]{:S(2)}) collective-permute-start(f32[1,256]{1,0:T(1,128)S(1)} %bitcast.206), channel_id=1, source_target_pairs={{0,1},{1,2},{2,3},{4,5},{5,6},{6,7},{8,9},{9,10},{10,11},{12,13},{... | collective-permute-start | bytes 3080 | tf_op jit(solution)/shard_map/ppermute | solution.py:19
  44.0 7.9 %collective-permute-start.7 = (f32[1,256]{1,0:T(1,128)S(1)}, f32[1,256]{1,0:T(1,128)S(1)}, u32[]{:S(2)}, u32[]{:S(2)}) collective-permute-start(f32[1,256]{1,0:T(1,128)S(1)} %bitcast.211), channel_id=1, source_target_pairs={{1,0},{2,1},{3,2},{5,4},{6,5},{7,6},{9,8},{10,9},{11,10},{13,12},{... | collective-permute-start | bytes 3080 | tf_op jit(solution)/shard_map/ppermute | solution.py:20
  45.4 6.8 %collective-permute-start.4 = (f32[1024]{0:T(1024)S(1)}, f32[1024]{0:T(1024)S(1)}, u32[]{:S(2)}, u32[]{:S(2)}) collective-permute-start(f32[1024]{0:T(1024)S(1)} %bitcast.192), channel_id=1, source_target_pairs={{28,0},{0,4},{4,8},{8,12},{12,16},{16,20},{20,24},{24,28},{29,1},{... | collective-permute-start | bytes 12296 | tf_op jit(solution)/shard_map/ppermute | solution.py:28
  45.5 6.7 %collective-permute-start.5 = (f32[1024]{0:T(1024)S(1)}, f32[1024]{0:T(1024)S(1)}, u32[]{:S(2)}, u32[]{:S(2)}) collective-permute-start(f32[1024]{0:T(1024)S(1)} %bitcast.189), channel_id=1, source_target_pairs={{4,0},{8,4},{12,8},{16,12},{20,16},{24,20},{28,24},{0,28},{5,1},{9... | collective-permute-start | bytes 12296 | tf_op jit(solution)/shard_map/ppermute | solution.py:28
  61.6 13.7 %copy-start.1 = (f32[256,1024]{1,0:T(8,128)}, f32[256,1024]{1,0:T(8,128)S(1)}, u32[]{:S(2)}) copy-start(f32[256,1024]{1,0:T(8,128)S(1)} %fusion.27) | copy-start | bytes 3145732
  63.3 12.1 %collective-permute-start.10 = (f32[1,256]{1,0:T(1,128)S(1)}, f32[1,256]{1,0:T(1,128)S(1)}, u32[]{:S(2)}, u32[]{:S(2)}) collective-permute-start(f32[1,256]{1,0:T(1,128)S(1)} %bitcast.216), channel_id=1, source_target_pairs={{0,1},{1,2},{2,3},{4,5},{5,6},{6,7},{8,9},{9,10},{10,11},{12,13},{... | collective-permute-start | bytes 3080 | tf_op jit(solution)/shard_map/ppermute | solution.py:19
  67.4 7.9 %collective-permute-start.11 = (f32[1,256]{1,0:T(1,128)S(1)}, f32[1,256]{1,0:T(1,128)S(1)}, u32[]{:S(2)}, u32[]{:S(2)}) collective-permute-start(f32[1,256]{1,0:T(1,128)S(1)} %bitcast.222), channel_id=1, source_target_pairs={{1,0},{2,1},{3,2},{5,4},{6,5},{7,6},{9,8},{10,9},{11,10},{13,12},{... | collective-permute-start | bytes 3080 | tf_op jit(solution)/shard_map/ppermute | solution.py:20
  68.7 6.8 %collective-permute-start.8 = (f32[1024]{0:T(1024)S(1)}, f32[1024]{0:T(1024)S(1)}, u32[]{:S(2)}, u32[]{:S(2)}) collective-permute-start(f32[1024]{0:T(1024)S(1)} %bitcast.195), channel_id=1, source_target_pairs={{28,0},{0,4},{4,8},{8,12},{12,16},{16,20},{20,24},{24,28},{29,1},{... | collective-permute-start | bytes 12296 | tf_op jit(solution)/shard_map/ppermute | solution.py:28
  68.8 6.7 %collective-permute-start.9 = (f32[1024]{0:T(1024)S(1)}, f32[1024]{0:T(1024)S(1)}, u32[]{:S(2)}, u32[]{:S(2)}) collective-permute-start(f32[1024]{0:T(1024)S(1)} %bitcast.198), channel_id=1, source_target_pairs={{4,0},{8,4},{12,8},{16,12},{20,16},{24,20},{28,24},{0,28},{5,1},{9... | collective-permute-start | bytes 12296 | tf_op jit(solution)/shard_map/ppermute | solution.py:28
  86.9 12.3 %collective-permute-start.14 = (f32[1,256]{1,0:T(1,128)S(1)}, f32[1,256]{1,0:T(1,128)S(1)}, u32[]{:S(2)}, u32[]{:S(2)}) collective-permute-start(f32[1,256]{1,0:T(1,128)S(1)} %bitcast.205), channel_id=1, source_target_pairs={{0,1},{1,2},{2,3},{4,5},{5,6},{6,7},{8,9},{9,10},{10,11},{12,13},{... | collective-permute-start | bytes 3080 | tf_op jit(solution)/shard_map/ppermute | solution.py:19
  91.2 7.9 %collective-permute-start.15 = (f32[1,256]{1,0:T(1,128)S(1)}, f32[1,256]{1,0:T(1,128)S(1)}, u32[]{:S(2)}, u32[]{:S(2)}) collective-permute-start(f32[1,256]{1,0:T(1,128)S(1)} %bitcast.208), channel_id=1, source_target_pairs={{1,0},{2,1},{3,2},{5,4},{6,5},{7,6},{9,8},{10,9},{11,10},{13,12},{... | collective-permute-start | bytes 3080 | tf_op jit(solution)/shard_map/ppermute | solution.py:20
  92.6 6.8 %collective-permute-start.12 = (f32[1024]{0:T(1024)S(1)}, f32[1024]{0:T(1024)S(1)}, u32[]{:S(2)}, u32[]{:S(2)}) collective-permute-start(f32[1024]{0:T(1024)S(1)} %bitcast.193), channel_id=1, source_target_pairs={{28,0},{0,4},{4,8},{8,12},{12,16},{16,20},{20,24},{24,28},{29,1},{... | collective-permute-start | bytes 12296 | tf_op jit(solution)/shard_map/ppermute | solution.py:28
  92.6 6.7 %collective-permute-start.13 = (f32[1024]{0:T(1024)S(1)}, f32[1024]{0:T(1024)S(1)}, u32[]{:S(2)}, u32[]{:S(2)}) collective-permute-start(f32[1024]{0:T(1024)S(1)} %bitcast.190), channel_id=1, source_target_pairs={{4,0},{8,4},{12,8},{16,12},{20,16},{24,20},{28,24},{0,28},{5,1},{9... | collective-permute-start | bytes 12296 | tf_op jit(solution)/shard_map/ppermute | solution.py:28
  108.7 13.9 %copy-start.2 = (f32[256,1024]{1,0:T(8,128)}, f32[256,1024]{1,0:T(8,128)S(1)}, u32[]{:S(2)}) copy-start(f32[256,1024]{1,0:T(8,128)S(1)} %fusion.37) | copy-start | bytes 3145732
  110.4 12.4 %collective-permute-start.18 = (f32[1,256]{1,0:T(1,128)S(1)}, f32[1,256]{1,0:T(1,128)S(1)}, u32[]{:S(2)}, u32[]{:S(2)}) collective-permute-start(f32[1,256]{1,0:T(1,128)S(1)} %bitcast.217), channel_id=1, source_target_pairs={{0,1},{1,2},{2,3},{4,5},{5,6},{6,7},{8,9},{9,10},{10,11},{12,13},{... | collective-permute-start | bytes 3080 | tf_op jit(solution)/shard_map/ppermute | solution.py:19
  114.8 7.9 %collective-permute-start.19 = (f32[1,256]{1,0:T(1,128)S(1)}, f32[1,256]{1,0:T(1,128)S(1)}, u32[]{:S(2)}, u32[]{:S(2)}) collective-permute-start(f32[1,256]{1,0:T(1,128)S(1)} %bitcast.224), channel_id=1, source_target_pairs={{1,0},{2,1},{3,2},{5,4},{6,5},{7,6},{9,8},{10,9},{11,10},{13,12},{... | collective-permute-start | bytes 3080 | tf_op jit(solution)/shard_map/ppermute | solution.py:20
  116.1 6.8 %collective-permute-start.16 = (f32[1024]{0:T(1024)S(1)}, f32[1024]{0:T(1024)S(1)}, u32[]{:S(2)}, u32[]{:S(2)}) collective-permute-start(f32[1024]{0:T(1024)S(1)} %bitcast.196), channel_id=1, source_target_pairs={{28,0},{0,4},{4,8},{8,12},{12,16},{16,20},{20,24},{24,28},{29,1},{... | collective-permute-start | bytes 12296 | tf_op jit(solution)/shard_map/ppermute | solution.py:28
  116.2 6.7 %collective-permute-start.17 = (f32[1024]{0:T(1024)S(1)}, f32[1024]{0:T(1024)S(1)}, u32[]{:S(2)}, u32[]{:S(2)}) collective-permute-start(f32[1024]{0:T(1024)S(1)} %bitcast.199), channel_id=1, source_target_pairs={{4,0},{8,4},{12,8},{16,12},{20,16},{24,20},{28,24},{0,28},{5,1},{9... | collective-permute-start | bytes 12296 | tf_op jit(solution)/shard_map/ppermute | solution.py:28
  134.3 11.0 %collective-permute-start.22 = (f32[1,256]{1,0:T(1,128)S(1)}, f32[1,256]{1,0:T(1,128)S(1)}, u32[]{:S(2)}, u32[]{:S(2)}) collective-permute-start(f32[1,256]{1,0:T(1,128)S(1)} %bitcast.207), channel_id=1, source_target_pairs={{0,1},{1,2},{2,3},{4,5},{5,6},{6,7},{8,9},{9,10},{10,11},{12,13},{... | collective-permute-start | bytes 3080 | tf_op jit(solution)/shard_map/ppermute | solution.py:19
  138.5 6.6 %collective-permute-start.23 = (f32[1,256]{1,0:T(1,128)S(1)}, f32[1,256]{1,0:T(1,128)S(1)}, u32[]{:S(2)}, u32[]{:S(2)}) collective-permute-start(f32[1,256]{1,0:T(1,128)S(1)} %bitcast.213), channel_id=1, source_target_pairs={{1,0},{2,1},{3,2},{5,4},{6,5},{7,6},{9,8},{10,9},{11,10},{13,12},{... | collective-permute-start | bytes 3080 | tf_op jit(solution)/shard_map/ppermute | solution.py:20
  139.8 5.6 %collective-permute-start.21 = (f32[1024]{0:T(1024)S(1)}, f32[1024]{0:T(1024)S(1)}, u32[]{:S(2)}, u32[]{:S(2)}) collective-permute-start(f32[1024]{0:T(1024)S(1)} %bitcast.191), channel_id=1, source_target_pairs={{4,0},{8,4},{12,8},{16,12},{20,16},{24,20},{28,24},{0,28},{5,1},{9... | collective-permute-start | bytes 12296 | tf_op jit(solution)/shard_map/ppermute | solution.py:28
  143.4 6.4 %collective-permute-start.20 = (f32[1024]{0:T(1024)S(1)}, f32[1024]{0:T(1024)S(1)}, u32[]{:S(2)}, u32[]{:S(2)}) collective-permute-start(f32[1024]{0:T(1024)S(1)} %bitcast.194), channel_id=1, source_target_pairs={{28,0},{0,4},{4,8},{8,12},{12,16},{16,20},{20,24},{24,28},{29,1},{... | collective-permute-start | bytes 12296 | tf_op jit(solution)/shard_map/ppermute | solution.py:28
  159.1 13.8 %copy-start.3 = (f32[256,1024]{1,0:T(8,128)}, f32[256,1024]{1,0:T(8,128)S(1)}, u32[]{:S(2)}) copy-start(f32[256,1024]{1,0:T(8,128)S(1)} %fusion.47) | copy-start | bytes 3145732
  160.8 12.3 %collective-permute-start.26 = (f32[1,256]{1,0:T(1,128)S(1)}, f32[1,256]{1,0:T(1,128)S(1)}, u32[]{:S(2)}, u32[]{:S(2)}) collective-permute-start(f32[1,256]{1,0:T(1,128)S(1)} %bitcast.218), channel_id=1, source_target_pairs={{0,1},{1,2},{2,3},{4,5},{5,6},{6,7},{8,9},{9,10},{10,11},{12,13},{... | collective-permute-start | bytes 3080 | tf_op jit(solution)/shard_map/ppermute | solution.py:19
  165.0 7.9 %collective-permute-start.27 = (f32[1,256]{1,0:T(1,128)S(1)}, f32[1,256]{1,0:T(1,128)S(1)}, u32[]{:S(2)}, u32[]{:S(2)}) collective-permute-start(f32[1,256]{1,0:T(1,128)S(1)} %bitcast.226), channel_id=1, source_target_pairs={{1,0},{2,1},{3,2},{5,4},{6,5},{7,6},{9,8},{10,9},{11,10},{13,12},{... | collective-permute-start | bytes 3080 | tf_op jit(solution)/shard_map/ppermute | solution.py:20
  166.4 6.8 %collective-permute-start.24 = (f32[1024]{0:T(1024)S(1)}, f32[1024]{0:T(1024)S(1)}, u32[]{:S(2)}, u32[]{:S(2)}) collective-permute-start(f32[1024]{0:T(1024)S(1)} %bitcast.197), channel_id=1, source_target_pairs={{28,0},{0,4},{4,8},{8,12},{12,16},{16,20},{20,24},{24,28},{29,1},{... | collective-permute-start | bytes 12296 | tf_op jit(solution)/shard_map/ppermute | solution.py:28
  166.5 6.7 %collective-permute-start.25 = (f32[1024]{0:T(1024)S(1)}, f32[1024]{0:T(1024)S(1)}, u32[]{:S(2)}, u32[]{:S(2)}) collective-permute-start(f32[1024]{0:T(1024)S(1)} %bitcast.200), channel_id=1, source_target_pairs={{4,0},{8,4},{12,8},{16,12},{20,16},{24,20},{28,24},{0,28},{5,1},{9... | collective-permute-start | bytes 12296 | tf_op jit(solution)/shard_map/ppermute | solution.py:28
  184.6 13.0 %collective-permute-start.30 = (f32[1,256]{1,0:T(1,128)S(1)}, f32[1,256]{1,0:T(1,128)S(1)}, u32[]{:S(2)}, u32[]{:S(2)}) collective-permute-start(f32[1,256]{1,0:T(1,128)S(1)} %bitcast.210), channel_id=1, source_target_pairs={{0,1},{1,2},{2,3},{4,5},{5,6},{6,7},{8,9},{9,10},{10,11},{12,13},{... | collective-permute-start | bytes 3080 | tf_op jit(solution)/shard_map/ppermute | solution.py:19
  189.8 7.7 %collective-permute-start.31 = (f32[1,256]{1,0:T(1,128)S(1)}, f32[1,256]{1,0:T(1,128)S(1)}, u32[]{:S(2)}, u32[]{:S(2)}) collective-permute-start(f32[1,256]{1,0:T(1,128)S(1)} %bitcast.215), channel_id=1, source_target_pairs={{1,0},{2,1},{3,2},{5,4},{6,5},{7,6},{9,8},{10,9},{11,10},{13,12},{... | collective-permute-start | bytes 3080 | tf_op jit(solution)/shard_map/ppermute | solution.py:20
  191.1 6.7 %collective-permute-start.28 = (f32[1024]{0:T(1024)S(1)}, f32[1024]{0:T(1024)S(1)}, u32[]{:S(2)}, u32[]{:S(2)}) collective-permute-start(f32[1024]{0:T(1024)S(1)} %bitcast.187), channel_id=1, source_target_pairs={{28,0},{0,4},{4,8},{8,12},{12,16},{16,20},{20,24},{24,28},{29,1},{... | collective-permute-start | bytes 12296 | tf_op jit(solution)/shard_map/ppermute | solution.py:28
  191.2 6.7 %collective-permute-start.29 = (f32[1024]{0:T(1024)S(1)}, f32[1024]{0:T(1024)S(1)}, u32[]{:S(2)}, u32[]{:S(2)}) collective-permute-start(f32[1024]{0:T(1024)S(1)} %bitcast.188), channel_id=1, source_target_pairs={{4,0},{8,4},{12,8},{16,12},{20,16},{24,20},{28,24},{0,28},{5,1},{9... | collective-permute-start | bytes 12296 | tf_op jit(solution)/shard_map/ppermute | solution.py:28
  207.2 1.0 copy-start.5
  209.5 23.2 %copy-start.8 = (s32[1024]{0:T(1024)S(1)}, s32[1024]{0:T(1024)}, u32[]{:S(2)}) copy-start(s32[1024]{0:T(1024)} %param.31) | copy-start | bytes 12292
  232.7 99.7 %all-reduce.2.cloned.1.call-start = ((), (), s32[]{:S(2)}) async-start(), calls=%async_computation.2 | async-start | bytes 262144 | tf_op jit(solution)/shard_map/psum | solution.py:158
Sparse Core Ops, SparseCore 0:
  232.8 25.6 reduce-scatter.1
  261.8 70.4 all-reduce.1
where the time goes:
time: 349 us; the launch traced here: 348 us
  waiting for transfers between devices  104 us (30%)
  local copies, waits for them, and re-layouts  85.8 us (25%)
  starting transfers between devices  80.9 us (23%)
  other arithmetic  47.1 us (13%)
  between operations  16.7 us (5%)
  blocking collectives  5.77 us (2%)
  matrix products  5.43 us (2%)
    psum x1, waiting for transfers between devices, on_device(): acoustic = lax.psum(share, 'pass')  73.9 us
    add x8, other arithmetic, relax(): keep * field + coeff[0] * below + coeff[1] * above + coeff[2] * left  39.5 us
    ppermute x16, starting transfers between devices, shifted(): return lax.ppermute(block, axis, route)  37.7 us
    gather x8, local copies, waits for them, and re-layouts, on_device(): mapped = jnp.take(jnp.where(half == 0, raw_low, raw_high), local_map)  36.2 us
    ppermute x8, starting transfers between devices, padded(): before = lax.ppermute(last, axis, up)  32.7 us
    reduce_scatter x1, waiting for transfers between devices, on_device(): lax.psum_scatter(blocks.reshape(per_cell * lax.axis_size('cell'), blocks....  25.6 us
    slice x8, local copies, waits for them, and re-layouts, relax(): above = jnp.concatenate([field[1:, :], ghost_high[None, :]], axis=0)  13.6 us
    slice x8, local copies, waits for them, and re-layouts, relax(): right = jnp.concatenate([field[:, 1:], rim[3][:, None]], axis=1)  13.3 us
  transfers between devices with their start and end apart: 34, of which 3 were waited for; matrix products, arithmetic and copies ran while one was open for 7% of the time, Pallas kernels for 0%

commit v1 on v0

--- a/solution.py
+++ b/solution.py
@@ -3,6 +3,7 @@
 import jax.numpy as jnp
 from jax import lax
 from jax.sharding import PartitionSpec as P
+from jax.lax import all_gather
 
 STEPS = 8
 GROUPS = 16
@@ -155,7 +156,7 @@
         scatter_dimension=0,
         tiled=True,
     )
-    acoustic = lax.psum(share, "pass")
+    acoustic = jnp.sum(all_gather(share, axis_name="pass"), axis=0)
     labels = jnp.arange(GROUPS, dtype=jnp.int32)
     my_groups = lax.dynamic_slice_in_dim(observer_group, cell_index * per_cell, per_cell)
     member = (my_groups[None, :] == labels[:, None]).astype(jnp.float32)

time: 349 us -> 316 us (0.905)
  waiting for transfers between devices: 104 us -> 72.4 us
    psum x1 -> x0, waiting for transfers between devices: 73.9 us -> none  [on_device(): acoustic = lax.psum(share, 'pass')]
    all_gather x0 -> x1, waiting for transfers between devices: none -> 42.2 us  [on_device(): acoustic = jnp.sum(all_gather(share, axis_name='pass'), axis=0)]
where the time goes in v1:
time: 316 us; the launch traced here: 315 us
  local copies, waits for them, and re-layouts  84 us (27%)
  starting transfers between devices  80.9 us (26%)
  waiting for transfers between devices  72.4 us (23%)
  other arithmetic  48.3 us (15%)
  between operations  16.7 us (5%)
  blocking collectives  5.77 us (2%)
  matrix products  4.59 us (1%)
    all_gather x1, waiting for transfers between devices, on_device(): acoustic = jnp.sum(all_gather(share, axis_name='pass'), axis=0)  42.2 us
    add x8, other arithmetic, relax(): keep * field + coeff[0] * below + coeff[1] * above + coeff[2] * left  39.4 us
    ppermute x16, starting transfers between devices, shifted(): return lax.ppermute(block, axis, route)  37.7 us
    gather x8, local copies, waits for them, and re-layouts, on_device(): mapped = jnp.take(jnp.where(half == 0, raw_low, raw_high), local_map)  36.2 us
    ppermute x8, starting transfers between devices, padded(): before = lax.ppermute(last, axis, up)  32.7 us
    reduce_scatter x1, waiting for transfers between devices, on_device(): lax.psum_scatter(blocks.reshape(per_cell * lax.axis_size('cell'), blocks....  25.8 us
    slice x8, local copies, waits for them, and re-layouts, relax(): above = jnp.concatenate([field[1:, :], ghost_high[None, :]], axis=0)  13.6 us
    slice x8, local copies, waits for them, and re-layouts, relax(): right = jnp.concatenate([field[:, 1:], rim[3][:, None]], axis=1)  13.3 us
  transfers between devices with their start and end apart: 34, of which 3 were waited for; matrix products, arithmetic and copies ran while one was open for 7% of the time, Pallas kernels for 0%

profile of v1, /device:TPU:0, one launch (start us, length us, event | category | flops | bytes accessed | tf_op | source)
XLA Modules:
  0.0 315.0 jit_solution(4284122152658025209)
XLA Ops:
  8.5 2.4 collective-permute-start.2
  10.9 1.3 collective-permute-start.3
  12.2 1.3 constant_dynamic-slice_fusion.12
  16.5 2.4 collective-permute-start
  18.9 3.1 collective-permute-start.1
  22.1 3.2 %fusion.109 = (f32[255,1024]{1,0:T(8,128)}, f32[255,1024]{1,0:T(8,128)}) fusion(f32[256,1024]{1,0:T(8,128)} %param.18), kind=kLoop, calls=%fused_computation.273 | loop fusion | bytes 4177920 | tf_op jit(solution)/shard_map/slice | solution.py:36
  25.3 1.7 fusion.108
  28.6 4.5 %gather_fusion.1 = f32[1024]{0:T(1024)S(1)} fusion(f32[1024]{0:T(1024)S(1)} %broadcast_select_fusion.7, s32[1024]{0:T(1024)S(1)} %fusion.82), kind=kCustom, calls=%fused_computation.clone | custom fusion | bytes 12288 | tf_op jit(solution)/shard_map/jit(_take)/gather | solution.py:122
  33.2 5.0 %fusion.22 = (f32[256,1024]{1,0:T(8,128)S(1)}, f32[256,1024]{1,0:T(8,128)S(1)}) fusion(f32[256,1024]{1,0:T(8,128)S(1)} %copy-done, f32[255,1024]{1,0:T(8,128)} %get-tuple-element.332, f32[1,1024]{1,0:T(1,128)S(1)} %bitcast.171, f32[1,1024]{1,0:T(1,128)S(1)} %bitcast.174, f32[255,1024]{1,0:T(8,128)} %get-tuple-element.331, ...), kind=kLoop, calls=%fused_computation.51 | loop fusion | flops 4718592 | bytes 12582912 | tf_op jit(solution)/shard_map/add | solution.py:41
  38.4 1.5 fusion.106
  39.9 4.0 %collective-permute-start.6 = (f32[1,256]{1,0:T(1,128)S(1)}, f32[1,256]{1,0:T(1,128)S(1)}, u32[]{:S(2)}, u32[]{:S(2)}) collective-permute-start(f32[1,256]{1,0:T(1,128)S(1)} %bitcast.208), channel_id=1, source_target_pairs={{0,1},{1,2},{2,3},{4,5},{5,6},{6,7},{8,9},{9,10},{10,11},{12,13},{... | collective-permute-start | bytes 3080 | tf_op jit(solution)/shard_map/ppermute | solution.py:20
  43.9 1.3 collective-permute-start.7
  45.4 4.7 %collective-permute-start.5 = (f32[1024]{0:T(1024)S(1)}, f32[1024]{0:T(1024)S(1)}, u32[]{:S(2)}, u32[]{:S(2)}) collective-permute-start(f32[1024]{0:T(1024)S(1)} %bitcast.191), channel_id=1, source_target_pairs={{4,0},{8,4},{12,8},{16,12},{20,16},{24,20},{28,24},{0,28},{5,1},{9... | collective-permute-start | bytes 12296 | tf_op jit(solution)/shard_map/ppermute | solution.py:29
  50.1 1.7 fusion.105
  52.1 4.5 %gather_fusion.2 = f32[1024]{0:T(1024)S(1)} fusion(f32[1024]{0:T(1024)S(1)} %broadcast_select_fusion.6, s32[1024]{0:T(1024)S(1)} %fusion.82), kind=kCustom, calls=%fused_computation.2.clone | custom fusion | bytes 12288 | tf_op jit(solution)/shard_map/jit(_take)/gather | solution.py:122
  56.7 4.8 %fusion.27 = f32[256,1024]{1,0:T(8,128)S(1)} fusion(f32[256,1024]{1,0:T(8,128)S(1)} %copy-done, f32[255,1024]{1,0:T(8,128)} %get-tuple-element.326, f32[1,1024]{1,0:T(1,128)S(1)} %bitcast.176, f32[1,1024]{1,0:T(1,128)S(1)} %bitcast.175, f32[255,1024]{1,0:T(8,128)} %get-tuple-element.325, f32[256,1023]{1,0:T(8,128)} %get-tuple-element.324, ...), kind=kLoop, calls=%fused_computation.60 | loop fusion | flops 3670016 | bytes 12582912 | tf_op jit(solution)/shard_map/add | solution.py:41
  61.7 1.5 fusion.103
  63.2 4.1 %collective-permute-start.10 = (f32[1,256]{1,0:T(1,128)S(1)}, f32[1,256]{1,0:T(1,128)S(1)}, u32[]{:S(2)}, u32[]{:S(2)}) collective-permute-start(f32[1,256]{1,0:T(1,128)S(1)} %bitcast.218), channel_id=1, source_target_pairs={{0,1},{1,2},{2,3},{4,5},{5,6},{6,7},{8,9},{9,10},{10,11},{12,13},{... | collective-permute-start | bytes 3080 | tf_op jit(solution)/shard_map/ppermute | solution.py:20
  67.3 1.3 collective-permute-start.11
  68.7 4.8 %collective-permute-start.9 = (f32[1024]{0:T(1024)S(1)}, f32[1024]{0:T(1024)S(1)}, u32[]{:S(2)}, u32[]{:S(2)}) collective-permute-start(f32[1024]{0:T(1024)S(1)} %bitcast.200), channel_id=1, source_target_pairs={{4,0},{8,4},{12,8},{16,12},{20,16},{24,20},{28,24},{0,28},{5,1},{9... | collective-permute-start | bytes 12296 | tf_op jit(solution)/shard_map/ppermute | solution.py:29
  73.5 1.7 fusion.102
  75.5 4.5 %gather_fusion.3 = f32[1024]{0:T(1024)S(1)} fusion(f32[1024]{0:T(1024)S(1)} %broadcast_select_fusion.5, s32[1024]{0:T(1024)S(1)} %fusion.82), kind=kCustom, calls=%fused_computation.3.clone | custom fusion | bytes 12288 | tf_op jit(solution)/shard_map/jit(_take)/gather | solution.py:122
  80.1 5.1 %fusion.32 = f32[256,1024]{1,0:T(8,128)S(1)} fusion(f32[256,1024]{1,0:T(8,128)S(1)} %copy-done, f32[255,1024]{1,0:T(8,128)} %get-tuple-element.320, f32[1,1024]{1,0:T(1,128)S(1)} %bitcast.178, f32[1,1024]{1,0:T(1,128)S(1)} %bitcast.177, f32[255,1024]{1,0:T(8,128)} %get-tuple-element.319, f32[256,1023]{1,0:T(8,128)} %get-tuple-element.318, ...), kind=kLoop, calls=%fused_computation.69 | loop fusion | flops 3670016 | bytes 12582912 | tf_op jit(solution)/shard_map/add | solution.py:41
  85.4 1.5 fusion.100
  86.8 4.3 %collective-permute-start.14 = (f32[1,256]{1,0:T(1,128)S(1)}, f32[1,256]{1,0:T(1,128)S(1)}, u32[]{:S(2)}, u32[]{:S(2)}) collective-permute-start(f32[1,256]{1,0:T(1,128)S(1)} %bitcast.207), channel_id=1, source_target_pairs={{0,1},{1,2},{2,3},{4,5},{5,6},{6,7},{8,9},{9,10},{10,11},{12,13},{... | collective-permute-start | bytes 3080 | tf_op jit(solution)/shard_map/ppermute | solution.py:20
  91.1 1.3 collective-permute-start.15
  92.6 4.7 %collective-permute-start.13 = (f32[1024]{0:T(1024)S(1)}, f32[1024]{0:T(1024)S(1)}, u32[]{:S(2)}, u32[]{:S(2)}) collective-permute-start(f32[1024]{0:T(1024)S(1)} %bitcast.192), channel_id=1, source_target_pairs={{4,0},{8,4},{12,8},{16,12},{20,16},{24,20},{28,24},{0,28},{5,1},{9... | collective-permute-start | bytes 12296 | tf_op jit(solution)/shard_map/ppermute | solution.py:29
  97.3 1.7 fusion.99
  99.3 4.5 %gather_fusion.4 = f32[1024]{0:T(1024)S(1)} fusion(f32[1024]{0:T(1024)S(1)} %broadcast_select_fusion.4, s32[1024]{0:T(1024)S(1)} %fusion.82), kind=kCustom, calls=%fused_computation.4.clone | custom fusion | bytes 12288 | tf_op jit(solution)/shard_map/jit(_take)/gather | solution.py:122
  103.8 4.8 %fusion.37 = f32[256,1024]{1,0:T(8,128)S(1)} fusion(f32[256,1024]{1,0:T(8,128)S(1)} %copy-done, f32[255,1024]{1,0:T(8,128)} %get-tuple-element.314, f32[1,1024]{1,0:T(1,128)S(1)} %bitcast.180, f32[1,1024]{1,0:T(1,128)S(1)} %bitcast.179, f32[255,1024]{1,0:T(8,128)} %get-tuple-element.313, f32[256,1023]{1,0:T(8,128)} %get-tuple-element.312, ...), kind=kLoop, calls=%fused_computation.78 | loop fusion | flops 3670016 | bytes 12582912 | tf_op jit(solution)/shard_map/add | solution.py:41
  108.9 1.5 fusion.97
  110.4 4.3 %collective-permute-start.18 = (f32[1,256]{1,0:T(1,128)S(1)}, f32[1,256]{1,0:T(1,128)S(1)}, u32[]{:S(2)}, u32[]{:S(2)}) collective-permute-start(f32[1,256]{1,0:T(1,128)S(1)} %bitcast.219), channel_id=1, source_target_pairs={{0,1},{1,2},{2,3},{4,5},{5,6},{6,7},{8,9},{9,10},{10,11},{12,13},{... | collective-permute-start | bytes 3080 | tf_op jit(solution)/shard_map/ppermute | solution.py:20
  114.7 1.3 collective-permute-start.19
  116.2 4.8 %collective-permute-start.17 = (f32[1024]{0:T(1024)S(1)}, f32[1024]{0:T(1024)S(1)}, u32[]{:S(2)}, u32[]{:S(2)}) collective-permute-start(f32[1024]{0:T(1024)S(1)} %bitcast.201), channel_id=1, source_target_pairs={{4,0},{8,4},{12,8},{16,12},{20,16},{24,20},{28,24},{0,28},{5,1},{9... | collective-permute-start | bytes 12296 | tf_op jit(solution)/shard_map/ppermute | solution.py:29
  120.9 1.7 fusion.96
  122.9 4.5 %gather_fusion.5 = f32[1024]{0:T(1024)S(1)} fusion(f32[1024]{0:T(1024)S(1)} %broadcast_select_fusion.3, s32[1024]{0:T(1024)S(1)} %fusion.82), kind=kCustom, calls=%fused_computation.5.clone | custom fusion | bytes 12288 | tf_op jit(solution)/shard_map/jit(_take)/gather | solution.py:122
  127.5 5.1 %fusion.42 = f32[256,1024]{1,0:T(8,128)S(1)} fusion(f32[256,1024]{1,0:T(8,128)S(1)} %copy-done, f32[255,1024]{1,0:T(8,128)} %get-tuple-element.308, f32[1,1024]{1,0:T(1,128)S(1)} %bitcast.182, f32[1,1024]{1,0:T(1,128)S(1)} %bitcast.181, f32[255,1024]{1,0:T(8,128)} %get-tuple-element.307, f32[256,1023]{1,0:T(8,128)} %get-tuple-element.306, ...), kind=kLoop, calls=%fused_computation.87 | loop fusion | flops 3670016 | bytes 12582912 | tf_op jit(solution)/shard_map/add | solution.py:41
  132.8 1.5 fusion.94
  134.3 4.2 %collective-permute-start.22 = (f32[1,256]{1,0:T(1,128)S(1)}, f32[1,256]{1,0:T(1,128)S(1)}, u32[]{:S(2)}, u32[]{:S(2)}) collective-permute-start(f32[1,256]{1,0:T(1,128)S(1)} %bitcast.209), channel_id=1, source_target_pairs={{0,1},{1,2},{2,3},{4,5},{5,6},{6,7},{8,9},{9,10},{10,11},{12,13},{... | collective-permute-start | bytes 3080 | tf_op jit(solution)/shard_map/ppermute | solution.py:20
  139.8 3.5 %collective-permute-start.21 = (f32[1024]{0:T(1024)S(1)}, f32[1024]{0:T(1024)S(1)}, u32[]{:S(2)}, u32[]{:S(2)}) collective-permute-start(f32[1024]{0:T(1024)S(1)} %bitcast.193), channel_id=1, source_target_pairs={{4,0},{8,4},{12,8},{16,12},{20,16},{24,20},{28,24},{0,28},{5,1},{9... | collective-permute-start | bytes 12296 | tf_op jit(solution)/shard_map/ppermute | solution.py:29
  143.4 1.7 fusion.93
  145.4 4.3 %collective-permute-done.20 = f32[1024]{0:T(1024)S(1)} collective-permute-done((f32[1024]{0:T(1024)S(1)}, f32[1024]{0:T(1024)S(1)}, u32[]{:S(2)}, u32[]{:S(2)}) %collective-permute-start.20) | collective-permute-done | bytes 4128 | tf_op jit(solution)/shard_map/ppermute | solution.py:29
  149.7 4.5 %gather_fusion.6 = f32[1024]{0:T(1024)S(1)} fusion(f32[1024]{0:T(1024)S(1)} %broadcast_select_fusion.2, s32[1024]{0:T(1024)S(1)} %fusion.82), kind=kCustom, calls=%fused_computation.6.clone | custom fusion | bytes 12288 | tf_op jit(solution)/shard_map/jit(_take)/gather | solution.py:122
  154.2 4.8 %fusion.47 = f32[256,1024]{1,0:T(8,128)S(1)} fusion(f32[256,1024]{1,0:T(8,128)S(1)} %copy-done, f32[255,1024]{1,0:T(8,128)} %get-tuple-element.302, f32[1,1024]{1,0:T(1,128)S(1)} %bitcast.184, f32[1,1024]{1,0:T(1,128)S(1)} %bitcast.183, f32[255,1024]{1,0:T(8,128)} %get-tuple-element.301, f32[256,1023]{1,0:T(8,128)} %get-tuple-element.300, ...), kind=kLoop, calls=%fused_computation.96 | loop fusion | flops 3670016 | bytes 12582912 | tf_op jit(solution)/shard_map/add | solution.py:41
  159.2 1.5 fusion.91
  160.7 4.3 %collective-permute-start.26 = (f32[1,256]{1,0:T(1,128)S(1)}, f32[1,256]{1,0:T(1,128)S(1)}, u32[]{:S(2)}, u32[]{:S(2)}) collective-permute-start(f32[1,256]{1,0:T(1,128)S(1)} %bitcast.220), channel_id=1, source_target_pairs={{0,1},{1,2},{2,3},{4,5},{5,6},{6,7},{8,9},{9,10},{10,11},{12,13},{... | collective-permute-start | bytes 3080 | tf_op jit(solution)/shard_map/ppermute | solution.py:20
  166.4 4.8 %collective-permute-start.25 = (f32[1024]{0:T(1024)S(1)}, f32[1024]{0:T(1024)S(1)}, u32[]{:S(2)}, u32[]{:S(2)}) collective-permute-start(f32[1024]{0:T(1024)S(1)} %bitcast.202), channel_id=1, source_target_pairs={{4,0},{8,4},{12,8},{16,12},{20,16},{24,20},{28,24},{0,28},{5,1},{9... | collective-permute-start | bytes 12296 | tf_op jit(solution)/shard_map/ppermute | solution.py:29
  171.2 1.7 fusion.90
  173.2 4.5 %gather_fusion.7 = f32[1024]{0:T(1024)S(1)} fusion(f32[1024]{0:T(1024)S(1)} %broadcast_select_fusion.1, s32[1024]{0:T(1024)S(1)} %fusion.82), kind=kCustom, calls=%fused_computation.7.clone | custom fusion | bytes 12288 | tf_op jit(solution)/shard_map/jit(_take)/gather | solution.py:122
  177.7 5.1 %fusion.52 = f32[256,1024]{1,0:T(8,128)S(1)} fusion(f32[256,1024]{1,0:T(8,128)S(1)} %copy-done, f32[255,1024]{1,0:T(8,128)} %get-tuple-element.296, f32[1,1024]{1,0:T(1,128)S(1)} %bitcast.186, f32[1,1024]{1,0:T(1,128)S(1)} %bitcast.185, f32[255,1024]{1,0:T(8,128)} %get-tuple-element.295, f32[256,1023]{1,0:T(8,128)} %get-tuple-element.294, ...), kind=kLoop, calls=%fused_computation.105 | loop fusion | flops 3670016 | bytes 12582912 | tf_op jit(solution)/shard_map/add | solution.py:41
  183.0 1.5 fusion.88
  184.6 5.1 %collective-permute-start.30 = (f32[1,256]{1,0:T(1,128)S(1)}, f32[1,256]{1,0:T(1,128)S(1)}, u32[]{:S(2)}, u32[]{:S(2)}) collective-permute-start(f32[1,256]{1,0:T(1,128)S(1)} %bitcast.212), channel_id=1, source_target_pairs={{0,1},{1,2},{2,3},{4,5},{5,6},{6,7},{8,9},{9,10},{10,11},{12,13},{... | collective-permute-start | bytes 3080 | tf_op jit(solution)/shard_map/ppermute | solution.py:20
  191.1 4.7 %collective-permute-start.29 = (f32[1024]{0:T(1024)S(1)}, f32[1024]{0:T(1024)S(1)}, u32[]{:S(2)}, u32[]{:S(2)}) collective-permute-start(f32[1024]{0:T(1024)S(1)} %bitcast.190), channel_id=1, source_target_pairs={{4,0},{8,4},{12,8},{16,12},{20,16},{24,20},{28,24},{0,28},{5,1},{9... | collective-permute-start | bytes 12296 | tf_op jit(solution)/shard_map/ppermute | solution.py:29
  195.8 1.7 fusion.87
  197.8 4.5 %gather_fusion.8 = f32[1024]{0:T(1024)S(1)} fusion(f32[1024]{0:T(1024)S(1)} %broadcast_select_fusion, s32[1024]{0:T(1024)S(1)} %fusion.82), kind=kCustom, calls=%fused_computation.8.clone | custom fusion | bytes 12288 | tf_op jit(solution)/shard_map/jit(_take)/gather | solution.py:122
  202.4 4.8 %fusion.57 = f32[256,1024]{1,0:T(8,128)S(1)} fusion(f32[256,1024]{1,0:T(8,128)S(1)} %copy-done, f32[255,1024]{1,0:T(8,128)} %get-tuple-element.290, f32[1,1024]{1,0:T(1,128)S(1)} %bitcast.173, f32[1,1024]{1,0:T(1,128)S(1)} %bitcast.172, f32[255,1024]{1,0:T(8,128)} %get-tuple-element.289, f32[256,1023]{1,0:T(8,128)} %get-tuple-element.288, ...), kind=kLoop, calls=%fused_computation.114 | loop fusion | flops 3670016 | bytes 12582912 | tf_op jit(solution)/shard_map/add | solution.py:41
  209.5 22.4 %while.13 = (s32[]{:T(128)}, f32[4,256,128]{2,1,0:T(8,128)}, f32[1024]{0:T(1024)S(1)}, f32[1,1024]{1,0:T(1,128)S(1)}, f32[]{:T(128)}, /*index=5*/f32[1024]{0:T(1...) while((s32[]{:T(128)}, f32[4,256,128]{2,1,0:T(8,128)}, ...), condition=%wide.region_1.3_spmd, body=%wide.region_0.2_spmd.sunk | while | flops 141568512 | bytes 2851517 | solution.py:150
  210.7 1.8 gather_fusion
  216.3 1.8 gather_fusion
  221.9 1.8 gather_fusion
  227.5 1.8 gather_fusion
  232.0 25.8 %reduce-scatter.2.cloned.1.call-done = f32[256,128]{1,0:T(8,128)} async-done(((f32[1024,128]{1,0:T(8,128)}), f32[256,128]{1,0:T(8,128)}) %reduce-scatter.2.cloned.1.call-update) | async-done | bytes 131088 | tf_op jit(solution)/shard_map/reduce_scatter | solution.py:153
  258.0 42.2 %all-gather.3.cloned.1.call-done = f32[2048,128]{1,0:T(8,128)} async-done(((f32[256,128]{1,0:T(8,128)}), f32[2048,128]{1,0:T(8,128)}) %all-gather.3.cloned.1.call-update) | async-done | bytes 1048592 | tf_op jit(solution)/shard_map/all_gather | solution.py:159
  301.7 5.8 %psum.7 = f32[16,128]{1,0:T(8,128)S(1)} all-reduce(f32[16,128]{1,0:T(8,128)S(1)} %fusion.66), channel_id=1, replica_groups=mesh['pass'=8,'cell'=4] {'cell'}, use_global_device_ids=true, to_apply=%region_4.6 | all-reduce | flops 2048 | bytes 16384 | tf_op jit(solution)/shard_map/psum | solution.py:167
  (214 shorter events, 30.3 us)
Async XLA Ops:
  7.2 18.1 %copy-start.4 = (f32[256,1024]{1,0:T(8,128)S(1)}, f32[256,1024]{1,0:T(8,128)}, u32[]{:S(2)}) copy-start(f32[256,1024]{1,0:T(8,128)} %param.18) | copy-start | bytes 3145732
  7.2 250.6 %reduce-scatter.2.cloned.1.call-start = ((), (), s32[]{:S(2)}) async-start(), calls=%async_computation.1 | async-start | bytes 655360 | tf_op jit(solution)/shard_map/reduce_scatter | solution.py:153
  8.5 19.9 %collective-permute-start.2 = (f32[1,256]{1,0:T(1,128)S(1)}, f32[1,256]{1,0:T(1,128)S(1)}, u32[]{:S(2)}, u32[]{:S(2)}) collective-permute-start(f32[1,256]{1,0:T(1,128)S(1)} %bitcast.204), channel_id=1, source_target_pairs={{0,1},{1,2},{2,3},{4,5},{5,6},{6,7},{8,9},{9,10},{10,11},{12,13},{... | collective-permute-start | bytes 3080 | tf_op jit(solution)/shard_map/ppermute | solution.py:20
  10.9 17.4 %collective-permute-start.3 = (f32[1,256]{1,0:T(1,128)S(1)}, f32[1,256]{1,0:T(1,128)S(1)}, u32[]{:S(2)}, u32[]{:S(2)}) collective-permute-start(f32[1,256]{1,0:T(1,128)S(1)} %bitcast.205), channel_id=1, source_target_pairs={{1,0},{2,1},{3,2},{5,4},{6,5},{7,6},{9,8},{10,9},{11,10},{13,12},{... | collective-permute-start | bytes 3080 | tf_op jit(solution)/shard_map/ppermute | solution.py:21
  16.5 12.0 %collective-permute-start = (f32[1024]{0:T(1024)S(1)}, f32[1024]{0:T(1024)S(1)}, u32[]{:S(2)}, u32[]{:S(2)}) collective-permute-start(f32[1024]{0:T(1024)S(1)} %bitcast.188), channel_id=1, source_target_pairs={{28,0},{0,4},{4,8},{8,12},{12,16},{16,20},{20,24},{24,28},{29,1},{... | collective-permute-start | bytes 12296 | tf_op jit(solution)/shard_map/ppermute | solution.py:29
  18.9 9.7 %collective-permute-start.1 = (f32[1024]{0:T(1024)S(1)}, f32[1024]{0:T(1024)S(1)}, u32[]{:S(2)}, u32[]{:S(2)}) collective-permute-start(f32[1024]{0:T(1024)S(1)} %bitcast.187), channel_id=1, source_target_pairs={{4,0},{8,4},{12,8},{16,12},{20,16},{24,20},{28,24},{0,28},{5,1},{9... | collective-permute-start | bytes 12296 | tf_op jit(solution)/shard_map/ppermute | solution.py:29
  22.0 4.9 %copy-start.10 = (s32[1,1024]{1,0:T(1,128)S(1)}, s32[1,1024]{1,0:T(1,128)}, u32[]{:S(2)}) copy-start(s32[1,1024]{1,0:T(1,128)} %param.23) | copy-start | bytes 12292
  22.0 5.0 %copy-start.11 = (f32[2,1024]{1,0:T(2,128)S(1)}, f32[2,1024]{1,0:T(2,128)}, u32[]{:S(2)}) copy-start(f32[2,1024]{1,0:T(2,128)} %param.28) | copy-start | bytes 24580
  22.0 5.1 %copy-start.12 = (f32[2,1024]{1,0:T(2,128)S(1)}, f32[2,1024]{1,0:T(2,128)}, u32[]{:S(2)}) copy-start(f32[2,1024]{1,0:T(2,128)} %param.27) | copy-start | bytes 24580
  22.0 5.1 %copy-start.13 = (f32[2,1024]{1,0:T(2,128)S(1)}, f32[2,1024]{1,0:T(2,128)}, u32[]{:S(2)}) copy-start(f32[2,1024]{1,0:T(2,128)} %param.25) | copy-start | bytes 24580
  22.0 5.2 %copy-start.14 = (f32[2,1024]{1,0:T(2,128)S(1)}, f32[2,1024]{1,0:T(2,128)}, u32[]{:S(2)}) copy-start(f32[2,1024]{1,0:T(2,128)} %param.26) | copy-start | bytes 24580
  22.0 5.2 %copy-start.15 = (f32[2,1024]{1,0:T(2,128)S(1)}, f32[2,1024]{1,0:T(2,128)}, u32[]{:S(2)}) copy-start(f32[2,1024]{1,0:T(2,128)} %param.29) | copy-start | bytes 24580
  22.0 5.2 %copy-start.8 = (f32[3,1024]{1,0:T(4,128)S(1)}, f32[3,1024]{1,0:T(4,128)}, u32[]{:S(2)}) copy-start(f32[3,1024]{1,0:T(4,128)} %param.30) | copy-start | bytes 36868
  25.3 7.9 %copy-start = (f32[256,1024]{1,0:T(8,128)S(1)}, f32[256,1024]{1,0:T(8,128)}, u32[]{:S(2)}) copy-start(f32[256,1024]{1,0:T(8,128)} %param.20) | copy-start | bytes 3145732
  38.2 7.1 %copy-start.7 = (f32[1,8,1024]{2,1,0:T(8,128)S(1)}, f32[1,8,1024]{2,1,0:T(8,128)}, u32[]{:S(2)}) copy-start(f32[1,8,1024]{2,1,0:T(8,128)} %param.21) | copy-start | bytes 98308
  39.9 12.1 %collective-permute-start.6 = (f32[1,256]{1,0:T(1,128)S(1)}, f32[1,256]{1,0:T(1,128)S(1)}, u32[]{:S(2)}, u32[]{:S(2)}) collective-permute-start(f32[1,256]{1,0:T(1,128)S(1)} %bitcast.208), channel_id=1, source_target_pairs={{0,1},{1,2},{2,3},{4,5},{5,6},{6,7},{8,9},{9,10},{10,11},{12,13},{... | collective-permute-start | bytes 3080 | tf_op jit(solution)/shard_map/ppermute | solution.py:20
  43.9 7.9 %collective-permute-start.7 = (f32[1,256]{1,0:T(1,128)S(1)}, f32[1,256]{1,0:T(1,128)S(1)}, u32[]{:S(2)}, u32[]{:S(2)}) collective-permute-start(f32[1,256]{1,0:T(1,128)S(1)} %bitcast.213), channel_id=1, source_target_pairs={{1,0},{2,1},{3,2},{5,4},{6,5},{7,6},{9,8},{10,9},{11,10},{13,12},{... | collective-permute-start | bytes 3080 | tf_op jit(solution)/shard_map/ppermute | solution.py:21
  45.3 6.8 %collective-permute-start.4 = (f32[1024]{0:T(1024)S(1)}, f32[1024]{0:T(1024)S(1)}, u32[]{:S(2)}, u32[]{:S(2)}) collective-permute-start(f32[1024]{0:T(1024)S(1)} %bitcast.194), channel_id=1, source_target_pairs={{28,0},{0,4},{4,8},{8,12},{12,16},{16,20},{20,24},{24,28},{29,1},{... | collective-permute-start | bytes 12296 | tf_op jit(solution)/shard_map/ppermute | solution.py:29
  45.4 6.7 %collective-permute-start.5 = (f32[1024]{0:T(1024)S(1)}, f32[1024]{0:T(1024)S(1)}, u32[]{:S(2)}, u32[]{:S(2)}) collective-permute-start(f32[1024]{0:T(1024)S(1)} %bitcast.191), channel_id=1, source_target_pairs={{4,0},{8,4},{12,8},{16,12},{20,16},{24,20},{28,24},{0,28},{5,1},{9... | collective-permute-start | bytes 12296 | tf_op jit(solution)/shard_map/ppermute | solution.py:29
  61.5 13.7 %copy-start.1 = (f32[256,1024]{1,0:T(8,128)}, f32[256,1024]{1,0:T(8,128)S(1)}, u32[]{:S(2)}) copy-start(f32[256,1024]{1,0:T(8,128)S(1)} %fusion.27) | copy-start | bytes 3145732
  63.2 12.1 %collective-permute-start.10 = (f32[1,256]{1,0:T(1,128)S(1)}, f32[1,256]{1,0:T(1,128)S(1)}, u32[]{:S(2)}, u32[]{:S(2)}) collective-permute-start(f32[1,256]{1,0:T(1,128)S(1)} %bitcast.218), channel_id=1, source_target_pairs={{0,1},{1,2},{2,3},{4,5},{5,6},{6,7},{8,9},{9,10},{10,11},{12,13},{... | collective-permute-start | bytes 3080 | tf_op jit(solution)/shard_map/ppermute | solution.py:20
  67.3 7.9 %collective-permute-start.11 = (f32[1,256]{1,0:T(1,128)S(1)}, f32[1,256]{1,0:T(1,128)S(1)}, u32[]{:S(2)}, u32[]{:S(2)}) collective-permute-start(f32[1,256]{1,0:T(1,128)S(1)} %bitcast.224), channel_id=1, source_target_pairs={{1,0},{2,1},{3,2},{5,4},{6,5},{7,6},{9,8},{10,9},{11,10},{13,12},{... | collective-permute-start | bytes 3080 | tf_op jit(solution)/shard_map/ppermute | solution.py:21
  68.6 6.8 %collective-permute-start.8 = (f32[1024]{0:T(1024)S(1)}, f32[1024]{0:T(1024)S(1)}, u32[]{:S(2)}, u32[]{:S(2)}) collective-permute-start(f32[1024]{0:T(1024)S(1)} %bitcast.197), channel_id=1, source_target_pairs={{28,0},{0,4},{4,8},{8,12},{12,16},{16,20},{20,24},{24,28},{29,1},{... | collective-permute-start | bytes 12296 | tf_op jit(solution)/shard_map/ppermute | solution.py:29
  68.7 6.7 %collective-permute-start.9 = (f32[1024]{0:T(1024)S(1)}, f32[1024]{0:T(1024)S(1)}, u32[]{:S(2)}, u32[]{:S(2)}) collective-permute-start(f32[1024]{0:T(1024)S(1)} %bitcast.200), channel_id=1, source_target_pairs={{4,0},{8,4},{12,8},{16,12},{20,16},{24,20},{28,24},{0,28},{5,1},{9... | collective-permute-start | bytes 12296 | tf_op jit(solution)/shard_map/ppermute | solution.py:29
  86.8 12.3 %collective-permute-start.14 = (f32[1,256]{1,0:T(1,128)S(1)}, f32[1,256]{1,0:T(1,128)S(1)}, u32[]{:S(2)}, u32[]{:S(2)}) collective-permute-start(f32[1,256]{1,0:T(1,128)S(1)} %bitcast.207), channel_id=1, source_target_pairs={{0,1},{1,2},{2,3},{4,5},{5,6},{6,7},{8,9},{9,10},{10,11},{12,13},{... | collective-permute-start | bytes 3080 | tf_op jit(solution)/shard_map/ppermute | solution.py:20
  91.1 7.9 %collective-permute-start.15 = (f32[1,256]{1,0:T(1,128)S(1)}, f32[1,256]{1,0:T(1,128)S(1)}, u32[]{:S(2)}, u32[]{:S(2)}) collective-permute-start(f32[1,256]{1,0:T(1,128)S(1)} %bitcast.210), channel_id=1, source_target_pairs={{1,0},{2,1},{3,2},{5,4},{6,5},{7,6},{9,8},{10,9},{11,10},{13,12},{... | collective-permute-start | bytes 3080 | tf_op jit(solution)/shard_map/ppermute | solution.py:21
  92.5 6.8 %collective-permute-start.12 = (f32[1024]{0:T(1024)S(1)}, f32[1024]{0:T(1024)S(1)}, u32[]{:S(2)}, u32[]{:S(2)}) collective-permute-start(f32[1024]{0:T(1024)S(1)} %bitcast.195), channel_id=1, source_target_pairs={{28,0},{0,4},{4,8},{8,12},{12,16},{16,20},{20,24},{24,28},{29,1},{... | collective-permute-start | bytes 12296 | tf_op jit(solution)/shard_map/ppermute | solution.py:29
  92.6 6.7 %collective-permute-start.13 = (f32[1024]{0:T(1024)S(1)}, f32[1024]{0:T(1024)S(1)}, u32[]{:S(2)}, u32[]{:S(2)}) collective-permute-start(f32[1024]{0:T(1024)S(1)} %bitcast.192), channel_id=1, source_target_pairs={{4,0},{8,4},{12,8},{16,12},{20,16},{24,20},{28,24},{0,28},{5,1},{9... | collective-permute-start | bytes 12296 | tf_op jit(solution)/shard_map/ppermute | solution.py:29
  108.6 13.9 %copy-start.2 = (f32[256,1024]{1,0:T(8,128)}, f32[256,1024]{1,0:T(8,128)S(1)}, u32[]{:S(2)}) copy-start(f32[256,1024]{1,0:T(8,128)S(1)} %fusion.37) | copy-start | bytes 3145732
  110.4 12.4 %collective-permute-start.18 = (f32[1,256]{1,0:T(1,128)S(1)}, f32[1,256]{1,0:T(1,128)S(1)}, u32[]{:S(2)}, u32[]{:S(2)}) collective-permute-start(f32[1,256]{1,0:T(1,128)S(1)} %bitcast.219), channel_id=1, source_target_pairs={{0,1},{1,2},{2,3},{4,5},{5,6},{6,7},{8,9},{9,10},{10,11},{12,13},{... | collective-permute-start | bytes 3080 | tf_op jit(solution)/shard_map/ppermute | solution.py:20
  114.7 7.9 %collective-permute-start.19 = (f32[1,256]{1,0:T(1,128)S(1)}, f32[1,256]{1,0:T(1,128)S(1)}, u32[]{:S(2)}, u32[]{:S(2)}) collective-permute-start(f32[1,256]{1,0:T(1,128)S(1)} %bitcast.226), channel_id=1, source_target_pairs={{1,0},{2,1},{3,2},{5,4},{6,5},{7,6},{9,8},{10,9},{11,10},{13,12},{... | collective-permute-start | bytes 3080 | tf_op jit(solution)/shard_map/ppermute | solution.py:21
  116.1 6.8 %collective-permute-start.16 = (f32[1024]{0:T(1024)S(1)}, f32[1024]{0:T(1024)S(1)}, u32[]{:S(2)}, u32[]{:S(2)}) collective-permute-start(f32[1024]{0:T(1024)S(1)} %bitcast.198), channel_id=1, source_target_pairs={{28,0},{0,4},{4,8},{8,12},{12,16},{16,20},{20,24},{24,28},{29,1},{... | collective-permute-start | bytes 12296 | tf_op jit(solution)/shard_map/ppermute | solution.py:29
  116.2 6.7 %collective-permute-start.17 = (f32[1024]{0:T(1024)S(1)}, f32[1024]{0:T(1024)S(1)}, u32[]{:S(2)}, u32[]{:S(2)}) collective-permute-start(f32[1024]{0:T(1024)S(1)} %bitcast.201), channel_id=1, source_target_pairs={{4,0},{8,4},{12,8},{16,12},{20,16},{24,20},{28,24},{0,28},{5,1},{9... | collective-permute-start | bytes 12296 | tf_op jit(solution)/shard_map/ppermute | solution.py:29
  134.3 11.0 %collective-permute-start.22 = (f32[1,256]{1,0:T(1,128)S(1)}, f32[1,256]{1,0:T(1,128)S(1)}, u32[]{:S(2)}, u32[]{:S(2)}) collective-permute-start(f32[1,256]{1,0:T(1,128)S(1)} %bitcast.209), channel_id=1, source_target_pairs={{0,1},{1,2},{2,3},{4,5},{5,6},{6,7},{8,9},{9,10},{10,11},{12,13},{... | collective-permute-start | bytes 3080 | tf_op jit(solution)/shard_map/ppermute | solution.py:20
  138.4 6.6 %collective-permute-start.23 = (f32[1,256]{1,0:T(1,128)S(1)}, f32[1,256]{1,0:T(1,128)S(1)}, u32[]{:S(2)}, u32[]{:S(2)}) collective-permute-start(f32[1,256]{1,0:T(1,128)S(1)} %bitcast.215), channel_id=1, source_target_pairs={{1,0},{2,1},{3,2},{5,4},{6,5},{7,6},{9,8},{10,9},{11,10},{13,12},{... | collective-permute-start | bytes 3080 | tf_op jit(solution)/shard_map/ppermute | solution.py:21
  139.8 5.6 %collective-permute-start.21 = (f32[1024]{0:T(1024)S(1)}, f32[1024]{0:T(1024)S(1)}, u32[]{:S(2)}, u32[]{:S(2)}) collective-permute-start(f32[1024]{0:T(1024)S(1)} %bitcast.193), channel_id=1, source_target_pairs={{4,0},{8,4},{12,8},{16,12},{20,16},{24,20},{28,24},{0,28},{5,1},{9... | collective-permute-start | bytes 12296 | tf_op jit(solution)/shard_map/ppermute | solution.py:29
  143.3 6.4 %collective-permute-start.20 = (f32[1024]{0:T(1024)S(1)}, f32[1024]{0:T(1024)S(1)}, u32[]{:S(2)}, u32[]{:S(2)}) collective-permute-start(f32[1024]{0:T(1024)S(1)} %bitcast.196), channel_id=1, source_target_pairs={{28,0},{0,4},{4,8},{8,12},{12,16},{16,20},{20,24},{24,28},{29,1},{... | collective-permute-start | bytes 12296 | tf_op jit(solution)/shard_map/ppermute | solution.py:29
  159.0 13.8 %copy-start.3 = (f32[256,1024]{1,0:T(8,128)}, f32[256,1024]{1,0:T(8,128)S(1)}, u32[]{:S(2)}) copy-start(f32[256,1024]{1,0:T(8,128)S(1)} %fusion.47) | copy-start | bytes 3145732
  160.7 12.3 %collective-permute-start.26 = (f32[1,256]{1,0:T(1,128)S(1)}, f32[1,256]{1,0:T(1,128)S(1)}, u32[]{:S(2)}, u32[]{:S(2)}) collective-permute-start(f32[1,256]{1,0:T(1,128)S(1)} %bitcast.220), channel_id=1, source_target_pairs={{0,1},{1,2},{2,3},{4,5},{5,6},{6,7},{8,9},{9,10},{10,11},{12,13},{... | collective-permute-start | bytes 3080 | tf_op jit(solution)/shard_map/ppermute | solution.py:20
  165.0 7.9 %collective-permute-start.27 = (f32[1,256]{1,0:T(1,128)S(1)}, f32[1,256]{1,0:T(1,128)S(1)}, u32[]{:S(2)}, u32[]{:S(2)}) collective-permute-start(f32[1,256]{1,0:T(1,128)S(1)} %bitcast.228), channel_id=1, source_target_pairs={{1,0},{2,1},{3,2},{5,4},{6,5},{7,6},{9,8},{10,9},{11,10},{13,12},{... | collective-permute-start | bytes 3080 | tf_op jit(solution)/shard_map/ppermute | solution.py:21
  166.3 6.8 %collective-permute-start.24 = (f32[1024]{0:T(1024)S(1)}, f32[1024]{0:T(1024)S(1)}, u32[]{:S(2)}, u32[]{:S(2)}) collective-permute-start(f32[1024]{0:T(1024)S(1)} %bitcast.199), channel_id=1, source_target_pairs={{28,0},{0,4},{4,8},{8,12},{12,16},{16,20},{20,24},{24,28},{29,1},{... | collective-permute-start | bytes 12296 | tf_op jit(solution)/shard_map/ppermute | solution.py:29
  166.4 6.7 %collective-permute-start.25 = (f32[1024]{0:T(1024)S(1)}, f32[1024]{0:T(1024)S(1)}, u32[]{:S(2)}, u32[]{:S(2)}) collective-permute-start(f32[1024]{0:T(1024)S(1)} %bitcast.202), channel_id=1, source_target_pairs={{4,0},{8,4},{12,8},{16,12},{20,16},{24,20},{28,24},{0,28},{5,1},{9... | collective-permute-start | bytes 12296 | tf_op jit(solution)/shard_map/ppermute | solution.py:29
  184.6 13.0 %collective-permute-start.30 = (f32[1,256]{1,0:T(1,128)S(1)}, f32[1,256]{1,0:T(1,128)S(1)}, u32[]{:S(2)}, u32[]{:S(2)}) collective-permute-start(f32[1,256]{1,0:T(1,128)S(1)} %bitcast.212), channel_id=1, source_target_pairs={{0,1},{1,2},{2,3},{4,5},{5,6},{6,7},{8,9},{9,10},{10,11},{12,13},{... | collective-permute-start | bytes 3080 | tf_op jit(solution)/shard_map/ppermute | solution.py:20
  189.8 7.8 %collective-permute-start.31 = (f32[1,256]{1,0:T(1,128)S(1)}, f32[1,256]{1,0:T(1,128)S(1)}, u32[]{:S(2)}, u32[]{:S(2)}) collective-permute-start(f32[1,256]{1,0:T(1,128)S(1)} %bitcast.217), channel_id=1, source_target_pairs={{1,0},{2,1},{3,2},{5,4},{6,5},{7,6},{9,8},{10,9},{11,10},{13,12},{... | collective-permute-start | bytes 3080 | tf_op jit(solution)/shard_map/ppermute | solution.py:21
  191.1 6.8 %collective-permute-start.28 = (f32[1024]{0:T(1024)S(1)}, f32[1024]{0:T(1024)S(1)}, u32[]{:S(2)}, u32[]{:S(2)}) collective-permute-start(f32[1024]{0:T(1024)S(1)} %bitcast.189), channel_id=1, source_target_pairs={{28,0},{0,4},{4,8},{8,12},{12,16},{16,20},{20,24},{24,28},{29,1},{... | collective-permute-start | bytes 12296 | tf_op jit(solution)/shard_map/ppermute | solution.py:29
  191.1 6.7 %collective-permute-start.29 = (f32[1024]{0:T(1024)S(1)}, f32[1024]{0:T(1024)S(1)}, u32[]{:S(2)}, u32[]{:S(2)}) collective-permute-start(f32[1024]{0:T(1024)S(1)} %bitcast.190), channel_id=1, source_target_pairs={{4,0},{8,4},{12,8},{16,12},{20,16},{24,20},{28,24},{0,28},{5,1},{9... | collective-permute-start | bytes 12296 | tf_op jit(solution)/shard_map/ppermute | solution.py:29
  207.2 1.0 copy-start.5
  209.5 48.4 %copy-start.9 = (s32[1024]{0:T(1024)S(1)}, s32[1024]{0:T(1024)}, u32[]{:S(2)}) copy-start(s32[1024]{0:T(1024)} %param.31) | copy-start | bytes 12292
  231.9 68.3 %all-gather.3.cloned.1.call-start = ((), (), s32[]{:S(2)}) async-start(), calls=%async_computation.2 | async-start | bytes 1179648 | tf_op jit(solution)/shard_map/all_gather | solution.py:159
  301.5 6.6 %copy-start.6 = (f32[256,128]{1,0:T(8,128)}, f32[256,128]{1,0:T(8,128)S(1)}, u32[]{:S(2)}) copy-start(f32[256,128]{1,0:T(8,128)S(1)} %reduce_sum.18) | copy-start | bytes 393220
Sparse Core Ops, SparseCore 0:
  232.1 25.7 reduce-scatter.1
  259.9 40.2 all-gather.2
